TPU v7x, 32 devices: a whole 2x2x4 slice. The times are simulated.
32 devices in a mesh: tm: 4 (over z), rows: 8 (over y, x, core).
Axes of the slice: x: 2, y: 2, z: 4, core: 2. Of those that a mesh axis runs over, the one named last changes fastest.
Arguments:
- feat_mid: bfloat16 [16, 64, 128, 256], P('tm', 'rows'), may hold values from -15 to 15
- gain_mid: float32 [256], replicated, may hold values from 0.1 to 1.9
- conv_mid: bfloat16 [3, 3, 3, 256, 256], replicated, may hold values from -0.078125 to 0.078125
- down_weight: bfloat16 [8, 256, 512], replicated, may hold values from -0.125 to 0.125
- wavelets: bfloat16 [8, 24, 32, 64], P('tm', None, 'rows'), may hold values from -6 to 6
- inject_weight: bfloat16 [24, 512], replicated, may hold values from -1.25 to 1.25
- gain_deep: float32 [512], replicated, may hold values from 0.1 to 1.9
- conv_deep: bfloat16 [3, 3, 3, 512, 512], replicated, may hold values from -0.0546875 to 0.0546875
Outputs:
- encoded: bfloat16 [8, 32, 64, 512], P('tm', 'rows')
All inputs are finite; a program needn't handle non-finite values.
Results may differ from a plain program's by a relative error of at most 0.0095.
Values may be sent and summed in bfloat16 or wider, within the bound.
No kernel may reach another device: no remote copies, remote signals or barrier semaphores. Data moves between devices by JAX's collectives and lax.ppermute only.
A program may use at most 256 MiB of HBM per device.

v0:
```python
import functools
import jax
import jax.numpy as jnp
from jax import lax
from jax.experimental import pallas as pl
from jax.experimental.pallas import tpu as pltpu
from jax.sharding import PartitionSpec as P

epsilon = 1e-06
haar_scale = 0.35355339059327373
PAD = 8
MIB = 1 << 20
WRAPS = (1, 1, 0)


def vmem():
    return pl.BlockSpec(memory_space=pltpu.VMEM)


def call(kernel, outs, ins, scratch=(), flops=0, limit=14, aliases=None, hbm=()):
    bytes_accessed = sum(int(a.size) * a.dtype.itemsize for a in ins)
    ins = [
        pltpu.with_memory_space_constraint(a, pltpu.HBM) if n in hbm else a
        for n, a in enumerate(ins)
    ]
    return pl.pallas_call(
        kernel,
        out_shape=outs,
        in_specs=[
            pl.BlockSpec(memory_space=pltpu.HBM) if n in hbm else vmem()
            for n in range(len(ins))
        ],
        out_specs=tuple(vmem() for _ in outs) if isinstance(outs, tuple) else vmem(),
        scratch_shapes=list(scratch),
        input_output_aliases=aliases or {},
        compiler_params=pltpu.CompilerParams(vmem_limit_bytes=limit * MIB),
        cost_estimate=pl.CostEstimate(
            flops=int(flops), bytes_accessed=bytes_accessed, transcendentals=0
        ),
    )(*ins)


def norm_act(values, gain):
    average = jnp.mean(values, axis=-1, keepdims=True)
    centred = values - average
    spread = jnp.mean(centred * centred, axis=-1, keepdims=True)
    half = centred * lax.rsqrt(spread + epsilon) * (0.5 * gain)
    return half + half * jnp.tanh(half)


def haar_cols(raw_ref, half):
    even = [raw_ref[:, q, pl.ds(0, half, stride=2), :] for q in range(raw_ref.shape[1])]
    odd = [raw_ref[:, q, pl.ds(1, half, stride=2), :] for q in range(raw_ref.shape[1])]
    return jnp.concatenate(even, -1), jnp.concatenate(odd, -1)


def prepare(values, gain, raw_ref, pad_ref, store, residual=None):
    _, width, channels = values.shape
    half = width // 2
    for q in range(channels // 128):
        raw_ref[:, q] = values[:, :, q * 128 : (q + 1) * 128].astype(jnp.float32)
    even, odd = haar_cols(raw_ref, half)
    if residual is not None:
        residual(0, even + odd)
        residual(1, even - odd)
    even, odd = norm_act(even, gain), norm_act(odd, gain)
    pad_ref[0, :, PAD : PAD + half, :] = odd
    pad_ref[1, :, PAD : PAD + half, :] = even
    store(0, pad_ref[0, :, PAD - 1 : PAD - 1 + half, :] - odd)
    store(1, even + odd)
    store(2, odd - even)
    store(3, even - pad_ref[1, :, PAD + 1 : PAD + 1 + half, :])


def clear_pads(pad_ref):
    rows, ext, channels = pad_ref.shape[1:]
    zero = jnp.zeros((rows, PAD, channels), jnp.float32)
    pad_ref[0, :, 0:PAD, :] = zero
    pad_ref[1, :, ext - PAD :, :] = zero


def norm_kernel(
    feat_hbm, gain_hbm, down_hbm, w_hbm, x_ref, res_ref, v_ref, g_ref, w_ref,
    feat_ref, gain_ref, down_ref, raw_ref, pad_ref, feat_sem, gain_sem, down_sem, w_sem,
    *, step
):
    frames, height, _, channels = feat_ref.shape
    feat_copies = [
        pltpu.make_async_copy(feat_hbm.at[f], feat_ref.at[f], feat_sem.at[f])
        for f in range(frames)
    ]
    w_copies = [pltpu.make_async_copy(w_hbm.at[a], w_ref.at[a], w_sem.at[a]) for a in range(3)]
    down_copy = pltpu.make_async_copy(down_hbm, down_ref, down_sem)
    gain_copy = pltpu.make_async_copy(gain_hbm, gain_ref, gain_sem)
    later_copies = [*w_copies, down_copy]
    for copy in (gain_copy, *feat_copies):
        copy.start()
    clear_pads(pad_ref)
    gain_copy.wait()
    gain = gain_ref[...]

    for f in range(frames):
        feat_copies[f].wait()
        if f == 0:
            for copy in later_copies:
                copy.start()

        def body(index, carry):
            h = index * step

            def store(t, value):
                x_ref[f, t, pl.ds(h + 1, step)] = value.astype(jnp.bfloat16)

            def residual(r, value):
                res_ref[f, r, pl.ds(h, step)] = value

            prepare(feat_ref[f, pl.ds(h, step)], gain, raw_ref, pad_ref, store, residual)
            return carry

        lax.fori_loop(0, height // step, body, 0)

    for a in range(3):
        w_copies[a].wait()

        def combine(b, carry):
            first, mid, last = (w_ref[a, b, c].astype(jnp.float32) for c in range(3))
            outer = first + last
            g_ref[a, b, 0] = (outer + mid).astype(jnp.bfloat16)
            g_ref[a, b, 1] = (outer - mid).astype(jnp.bfloat16)
            return carry

        lax.fori_loop(0, 3, combine, 0)

    down_copy.wait()
    rows = 32

    def fold(index, carry):
        r = pl.multiple_of(index * rows, rows)
        parts = [down_ref[s, pl.ds(r, rows), :].astype(jnp.float32) for s in range(8)]
        for bit in (4, 2):
            parts = [
                parts[s] + parts[s + bit] if not s & bit else parts[s - bit] - parts[s]
                for s in range(8)
            ]
        for s in range(8):
            v_ref[s, pl.ds(r, rows), :] = parts[s].astype(jnp.bfloat16)
        return carry

    lax.fori_loop(0, channels // rows, fold, 0)


def conv_pair(pair, x_ref, w_ref, g_ref, res_ref, v_ref, lev_ref, group):
    frames, _, ext, half, channels = x_ref.shape
    deep_rows = (ext - 2) // 2

    for index in range(deep_rows // group):
        start = 2 * group * index
        for i in range(2):
            f = 2 * pair + i
            taps = [a for a in range(3) if 0 <= f + a - 2 < frames]
            sums = []
            for t in range(4):
                total = None
                for a in taps:
                    for b in range(3):
                        rows = x_ref[f + a - 2, t, pl.ds(start + b, 2 * group)].reshape(
                            2 * group * half, channels
                        )
                        weight = (
                            w_ref[a, b, 0], g_ref[a, b, 0], g_ref[a, b, 1], w_ref[a, b, 2]
                        )[t]
                        part = jnp.dot(rows, weight, preferred_element_type=jnp.float32)
                        total = part if total is None else total + part
                sums.append(total)
            pieces = (sums[0] - sums[3] + sums[1], sums[0] + sums[3] + sums[2])
            for r in range(2):
                level = pieces[r].reshape(2 * group, half, channels)
                if res_ref is not None:
                    level = level + res_ref[f, r, pl.ds(start, 2 * group)]
                level = level.astype(jnp.bfloat16)
                for row in range(2 * group):
                    lev_ref[4 * i + 2 * (row % 2) + r, index * group + row // 2] = level[row]
    total = None
    for s in range(8):
        part = jnp.dot(
            lev_ref[s].reshape(deep_rows * half, channels),
            v_ref[s],
            preferred_element_type=jnp.float32,
        )
        total = part if total is None else total + part
    return total * haar_scale


def carry_kernel(
    x_in, near_ref, far_ref, gain_ref, w_ref, g_ref, v_ref, x_ref, out_ref,
    lev_ref, raw_ref, pad_ref, *, group
):
    frames, _, ext, _, _ = x_ref.shape
    gain = gain_ref[...]
    clear_pads(pad_ref)

    def halos(first, count):
        sides = by_side(near_ref[first : first + count, 0], far_ref[first : first + count, 0])
        for row, values in zip((0, ext - 1), sides):

            def store(t, value):
                for f in range(count):
                    x_ref[first + f, t, row] = value[f].astype(jnp.bfloat16)

            prepare(
                values, gain, raw_ref.at[first : first + count],
                pad_ref.at[:, first : first + count], store
            )

    halos(frames - 2, 2)
    projected = conv_pair(frames // 2, x_ref, w_ref, g_ref, None, v_ref, lev_ref, group)
    out_ref[...] = projected.reshape(out_ref.shape).astype(out_ref.dtype)
    halos(0, frames - 2)


def own_kernel(*refs, pair, extra, group, later):
    x_ref, res_ref, w_ref, g_ref, v_ref, wav_ref, inj_ref, gain_ref = refs[:8]
    carried_ref = refs[8] if extra else None
    later_refs = refs[8 + extra : 8 + extra + later]
    outs = refs[8 + extra + later :]
    deep_ref, lev_ref = outs[0], outs[-1]
    normed_refs = outs[1:-1]
    gain = gain_ref[...]
    injected = [
        lax.dot_general(
            wav_ref[pair, :, h, :],
            inj_ref[...],
            (((0,), (0,)), ((), ())),
            preferred_element_type=jnp.float32,
        )
        for h in range(wav_ref.shape[2])
    ]
    for ref, out in zip(later_refs, normed_refs[1:]):
        out[...] = norm_act(ref[...], gain).astype(out.dtype)
    value = conv_pair(pair, x_ref, w_ref, g_ref, res_ref, v_ref, lev_ref, group)
    value = value + jnp.concatenate(injected, 0)
    if extra:
        value = value + arrived(carried_ref[...].reshape(value.shape))
    deep_ref[...] = value.reshape(deep_ref.shape)
    if extra:
        normed_refs[0][...] = norm_act(value, gain).reshape(deep_ref.shape).astype(jnp.bfloat16)


def shifted(z_ref, sums):
    rows, ext = z_ref.shape[1:3]
    width = ext - 2 * PAD
    for c in range(3):
        z_ref[c, :, PAD : PAD + width, :] = sums[c].reshape(rows, width, -1)
    return (
        z_ref[0, :, PAD - 1 : PAD - 1 + width, :]
        + z_ref[1, :, PAD : PAD + width, :]
        + z_ref[2, :, PAD + 1 : PAD + 1 + width, :]
    )


def clear_columns(z_ref):
    rows, ext, channels = z_ref.shape[1:]
    zero = jnp.zeros((rows, PAD, channels), jnp.float32)
    z_ref[0, :, 0:PAD, :] = zero
    z_ref[2, :, ext - PAD :, :] = zero


def dot(rows, weight):
    return jnp.dot(rows, weight, preferred_element_type=jnp.float32)


def deep_conv(targets, ext_ref, w_ref, z_ref):
    frames, ext, width, channels = ext_ref.shape
    rows = ext - 2
    for target in targets:
        sums = []
        for c in range(3):
            total = None
            for a in range(3):
                source = target + a - 2
                if 0 <= source < frames:
                    for b in range(3):
                        part = dot(
                            ext_ref[source, b : b + rows].reshape(rows * width, channels),
                            w_ref[a, b, c],
                        )
                        total = part if total is None else total + part
            sums.append(total)
        yield target, shifted(z_ref, sums)


def deep_carry(rows, w_ref, z_ref, out_ref):
    both, last = [], []
    for c in range(3):
        first_tap, mid_tap = None, None
        for b in range(3):
            before, latest = rows(0, b), rows(1, b)
            part = dot(jnp.concatenate([before, latest], 0), w_ref[0, b, c])
            first_tap = part if first_tap is None else first_tap + part
            part = dot(latest, w_ref[1, b, c])
            mid_tap = part if mid_tap is None else mid_tap + part
        half = mid_tap.shape[0]
        both.append(first_tap[:half] + mid_tap)
        last.append(first_tap[half:])
    out_ref[0] = shifted(z_ref, both).astype(out_ref.dtype)
    out_ref[1] = shifted(z_ref, last).astype(out_ref.dtype)


def fill_ext(ext_ref, own_refs, near_ref, far_ref):
    frames, ext, _, _ = ext_ref.shape
    for f in range(frames):
        ext_ref[f, 1 : ext - 1] = own_refs[f][...]
        ext_ref[f, 0], ext_ref[f, ext - 1] = by_side(near_ref[f, 0], far_ref[f, 0])


def inner_carry_kernel(before_ref, latest_ref, w_ref, out_ref, z_ref):
    inner, _, channels = z_ref.shape[1:]
    clear_columns(z_ref)

    def rows(f, b):
        return (before_ref, latest_ref)[f][b : b + inner].reshape(-1, channels)

    deep_carry(rows, w_ref, z_ref, out_ref)


def outer_carry_kernel(
    before_ref, latest_ref, near_ref, far_ref, w_ref, out_ref, halo_ref, z_ref
):
    count = before_ref.shape[0]
    clear_columns(z_ref)
    first = near_ref.shape[0] - 2
    for f in range(2):
        halo_ref[f, 0], halo_ref[f, 1] = by_side(near_ref[first + f, 0], far_ref[first + f, 0])

    def one(f, r):
        if r < 0:
            return halo_ref[f, 0]
        if r >= count:
            return halo_ref[f, 1]
        return (before_ref, latest_ref)[f][r]

    def rows(f, b):
        return jnp.concatenate([one(f, b - 1), one(f, count + b - 2)], 0)

    deep_carry(rows, w_ref, z_ref, out_ref)


def deep_own_kernel(*refs, frames):
    own_refs = refs[:frames]
    feat_refs = refs[frames : 2 * frames]
    near_ref, far_ref, w_ref, out_ref, ext_ref, z_ref = refs[2 * frames :]
    clear_columns(z_ref)
    fill_ext(ext_ref, own_refs, near_ref, far_ref)
    for target, value in deep_conv(range(frames), ext_ref, w_ref, z_ref):
        out_ref[target] = value + feat_refs[target][...]


def arrived(values):
    values = values.astype(jnp.float32)
    return jnp.where(lax.axis_index("tm") == 0, jnp.zeros_like(values), values)


def join_kernel(own_ref, inner_ref, outer_ref, out_ref):
    frames, rows = own_ref.shape[:2]
    for f in range(frames):
        if f < 2:
            out_ref[f, 1 : rows - 1] = (
                own_ref[f, 1 : rows - 1] + arrived(inner_ref[f])
            ).astype(out_ref.dtype)
            for n, r in enumerate((0, rows - 1)):
                out_ref[f, r] = (own_ref[f, r] + arrived(outer_ref[f, n])).astype(out_ref.dtype)
        else:
            out_ref[f] = own_ref[f].astype(out_ref.dtype)


def chain(axis, wrap):
    count = lax.axis_size(axis)
    return [(i, (i + 1) % count) for i in range(count - 1 + wrap)]


def neighbours(axis):
    count = lax.axis_size(axis)
    routes = []
    for first in range(2):
        partner = {}
        for i in range(first, count - 1, 2):
            partner[i], partner[i + 1] = i + 1, i
        routes.append([(i, partner.get(i, i)) for i in range(count)])
    return routes


def by_side(near, far):
    index, count = lax.axis_index("rows"), lax.axis_size("rows")
    odd = lax.rem(index, 2) == 1
    above = jnp.where(odd, near, far)
    below = jnp.where(odd, far, near)
    above = jnp.where(index == 0, jnp.zeros_like(above), above)
    return above, jnp.where(index == count - 1, jnp.zeros_like(below), below)


def exchange(first_rows, last_rows):
    odd = lax.rem(lax.axis_index("rows"), 2) == 1
    routes = neighbours("rows")
    near = lax.ppermute(jnp.where(odd, first_rows, last_rows), "rows", routes[0])
    far = lax.ppermute(jnp.where(odd, last_rows, first_rows), "rows", routes[1])
    return near, far


def on_device(
    feat_mid, gain_mid, conv_mid, down_weight, wavelets, inject_weight, gain_deep, conv_deep
):
    frames, height, width, channels = feat_mid.shape
    deep_channels = down_weight.shape[-1]
    deep_frames, deep_rows, half = frames // 2, height // 2, width // 2
    group = 2 if deep_rows % 2 == 0 else 1
    bf16, f32 = jnp.bfloat16, jnp.float32
    shape = jax.ShapeDtypeStruct
    local = pltpu.VMEM
    gain_mid = gain_mid.reshape(1, -1)
    gain_deep = gain_deep.reshape(1, -1)

    near, far = exchange(feat_mid[:, :1], feat_mid[:, height - 1 :])
    x_shape = local((frames, 4, height + 2, half, channels), bf16)
    step = 4
    sem = pltpu.SemaphoreType.DMA
    x, residual, folded, mixed, conv_mid = call(
        functools.partial(norm_kernel, step=step),
        (
            x_shape,
            local((frames, 2, height, half, channels), f32),
            local(down_weight.shape, bf16),
            local((3, 3, 2) + conv_mid.shape[-2:], bf16),
            local(conv_mid.shape, bf16),
        ),
        (feat_mid, gain_mid, down_weight, conv_mid),
        (
            pltpu.VMEM(feat_mid.shape, bf16),
            pltpu.VMEM(gain_mid.shape, f32),
            pltpu.VMEM(down_weight.shape, bf16),
            pltpu.VMEM((step, channels // 128, width, 128), f32),
            pltpu.VMEM((2, step, half + 2 * PAD, channels), f32),
            sem((frames,)),
            sem(()),
            sem(()),
            sem((3,)),
        ),
        flops=5e9,
        hbm=(0, 1, 2, 3),
    )
    lev = pltpu.VMEM((8, deep_rows, half, channels), bf16)
    tap = 2 * height * width * channels * channels * 6
    proj = 2 * deep_rows * half * 8 * channels * deep_channels

    x, carry = call(
        functools.partial(carry_kernel, group=group),
        (x_shape, shape((deep_rows, half, deep_channels), bf16)),
        (x, near, far, gain_mid, conv_mid, mixed, folded),
        (
            lev,
            pltpu.VMEM((frames, channels // 128, width, 128), f32),
            pltpu.VMEM((2, frames, half + 2 * PAD, channels), f32),
        ),
        flops=3 * tap + proj,
        aliases={0: 0},
    )
    carried = lax.ppermute(carry, "tm", chain("tm", WRAPS[0]))
    deep = [None] * deep_frames
    for pair in reversed(range(deep_frames)):
        extra = pair == 0
        later = tuple(deep[1:]) if extra else ()
        made = call(
            functools.partial(own_kernel, pair=pair, extra=extra, group=group, later=len(later)),
            (shape((deep_rows, half, deep_channels), f32),)
            + (shape((deep_rows, half, deep_channels), bf16),) * (extra * deep_frames),
            (x, residual, conv_mid, mixed, folded, wavelets, inject_weight, gain_deep)
            + ((carried,) if extra else ())
            + later,
            (lev,),
            flops=(3 if extra else 6) * tap + proj,
        )
        deep[pair] = made[0]
    normed = made[1:]
    near, far = exchange(
        jnp.stack([n[:1] for n in normed]), jnp.stack([n[deep_rows - 1 :] for n in normed])
    )
    ext = pltpu.VMEM((deep_frames, deep_rows + 2, half, deep_channels), bf16)
    z = pltpu.VMEM((3, deep_rows, half + 2 * PAD, deep_channels), f32)
    tap = 2 * deep_rows * half * deep_channels * deep_channels * 9
    inner_z = pltpu.VMEM((3, deep_rows - 2, half + 2 * PAD, deep_channels), f32)
    outer_z = pltpu.VMEM((3, 2, half + 2 * PAD, deep_channels), f32)
    inner = call(
        inner_carry_kernel,
        shape((2, deep_rows - 2, half, deep_channels), bf16),
        (*normed[-2:], conv_deep),
        (inner_z,),
        flops=3 * tap * (deep_rows - 2) / deep_rows,
    )
    inner = lax.ppermute(inner, "tm", chain("tm", WRAPS[1]))
    outer = call(
        outer_carry_kernel,
        shape((2, 2, half, deep_channels), bf16),
        (*normed[-2:], near, far, conv_deep),
        (pltpu.VMEM((2, 2, half, deep_channels), bf16), outer_z),
        flops=3 * tap * 2 / deep_rows,
    )
    outer = lax.ppermute(outer, "tm", chain("tm", WRAPS[2]))
    own = call(
        functools.partial(deep_own_kernel, frames=deep_frames),
        shape((deep_frames, deep_rows, half, deep_channels), f32),
        (*normed, *deep, near, far, conv_deep),
        (ext, z),
        flops=(3 * deep_frames - 3) * tap,
    )
    return call(
        join_kernel,
        shape((deep_frames, deep_rows, half, deep_channels), bf16),
        (own, inner, outer),
    )


def solution(mesh):
    return jax.shard_map(
        on_device,
        mesh=mesh,
        in_specs=(
            P("tm", "rows", None, None),
            P(),
            P(),
            P(),
            P("tm", None, "rows", None),
            P(),
            P(),
            P(),
        ),
        out_specs=P("tm", "rows", None, None),
        check_vma=False,
    )
```

profile of v0, /device:TPU:0, one launch (start us, length us, event | category | flops | bytes accessed | tf_op | source)
XLA Modules:
  0.0 49.3 jit_solution(16763910481308623886)
XLA Ops:
  0.0 1.1 %broadcast_select_fusion = (bf16[4,1,128,256]{3,2,1,0:T(8,128)(2,1)S(1)}, bf16[4,1,128,256]{3,2,1,0:T(8,128)(2,1)S(1)}) fusion(pred[]{:T(512)S(6)} %eq.4, bf16[4,8,128,256]{3,2,1,0:T(8,128)(2,1)} %feat_hbm.1), kind=kLoop, calls=%fused_computation | loop fusion | flops 262144 | bytes 1048577 | tf_op jit(solution)/shard_map/jit(_where)/select_n | solution.py:405
  1.1 0.7 %collective-permute-start.1 = (bf16[4,1,128,256]{3,2,1,0:T(8,128)(2,1)S(1)}, bf16[4,1,128,256]{3,2,1,0:T(8,128)(2,1)S(1)}, u32[]{:S(2)}, u32[]{:S(2)}) collective-permute-start(bf16[4,1,128,256]{3,2,1,0:T(8,128)(2,1)S(1)} %get-tuple-element.25), channel_id=1, source_target_pairs={{0,0},{1,2},{2,1},{3,4},{4,3},{5,6},{6,5},{7,7},{8,8},{9,10},{10,9... | collective-permute-start | bytes 786440 | tf_op jit(solution)/shard_map/ppermute | solution.py:405
  1.8 4.4 %collective-permute-start = (bf16[4,1,128,256]{3,2,1,0:T(8,128)(2,1)S(1)}, bf16[4,1,128,256]{3,2,1,0:T(8,128)(2,1)S(1)}, u32[]{:S(2)}, u32[]{:S(2)}) collective-permute-start(bf16[4,1,128,256]{3,2,1,0:T(8,128)(2,1)S(1)} %get-tuple-element.26), channel_id=1, source_target_pairs={{0,1},{1,0},{2,3},{3,2},{4,5},{5,4},{6,7},{7,6},{8,9},{9,8},{10,11... | collective-permute-start | bytes 786440 | tf_op jit(solution)/shard_map/ppermute | solution.py:404
  6.1 0.0 copy-start.3
  6.1 6.4 %shard_map.82 = (bf16[4,4,10,64,256]{4,3,2,1,0:T(8,128)(2,1)S(1)}, f32[4,2,8,64,256]{4,3,2,1,0:T(8,128)S(1)}, bf16[8,256,512]{2,1,0:T(8,128)(2,1)S(1)}, bf16[3,3...) custom-call(bf16[4,8,128,256]{3,2,1,0:T(8,128)(2,1)} %feat_hbm.1, f32[1,256]{1,0:T(1,128)} %bitcast.14, ...), custom_call_target="tpu_custom_call" | custom-call | flops 5000000000 | bytes 7734272 | tf_op jit(solution)/shard_map/pallas_call | solution.py:26
  12.5 0.0 collective-permute-done.1.far_ref
  12.5 0.0 collective-permute-done.near_ref
  12.5 0.0 copy-done.3
  12.5 0.0 copy-start
  12.5 0.0 copy-start.1
  12.6 0.0 copy-start.2
  12.6 3.6 %shard_map.83 = (bf16[4,4,10,64,256]{4,3,2,1,0:T(8,128)(2,1)S(1)}, bf16[4,64,512]{2,1,0:T(8,128)(2,1)S(1)}) custom-call(bf16[4,4,10,64,256]{4,3,2,1,0:T(8,128)(2,1)S(1)} %get-tuple-element.15.x_in, bf16[4,1,128,256]{3,2,1,0:T(8,128)(2,1)S(1)} %collective-permute-done.near_ref, ...), custom_call_target="tpu_custom_call", output_to_operand_aliasing={{0}: (0, {})} | custom-call | flops 2952790016 | bytes 13763584 | tf_op jit(solution)/shard_map/pallas_call | solution.py:26
  16.2 1.8 %collective-permute-start.2 = (bf16[4,64,512]{2,1,0:T(8,128)(2,1)S(1)}, bf16[4,64,512]{2,1,0:T(8,128)(2,1)S(1)}, u32[]{:S(2)}, u32[]{:S(2)}) collective-permute-start(bf16[4,64,512]{2,1,0:T(8,128)(2,1)S(1)} %get-tuple-element.21), channel_id=1, source_target_pairs={{0,8},{8,16},{16,24},{24,0},{1,9},{9,17},{17,25},{25,1},{2,10},{10... | collective-permute-start | bytes 786440 | tf_op jit(solution)/shard_map/ppermute | solution.py:466
  18.0 0.0 copy-done
  18.0 0.0 copy-done.1
  18.0 0.0 copy-done.2
  18.0 0.0 slice-start
  18.0 0.0 slice-start.1
  18.0 0.0 slice-start.2
  18.0 6.0 %shard_map.84.refs_9_.refs_3_ = f32[4,64,512]{2,1,0:T(8,128)S(1)} custom-call(bf16[4,4,10,64,256]{4,3,2,1,0:T(8,128)(2,1)S(1)} %get-tuple-element.19.refs_0_, f32[4,2,8,64,256]{4,3,2,1,0:T(8,128)S(1)} %get-tuple-element.20.refs_1_, bf16[3,3,3,256,256]{4,3,2,1,0:T(8,128)(2,1)S(1)} %get-tuple-element.16.w_ref.refs_2_, ...), custom_call_target="tpu_custom_call" | custom-call | flops 5368709120 | bytes 17483776 | tf_op jit(solution)/shard_map/pallas_call | solution.py:26
  24.1 0.0 slice-start.3
  24.1 2.4 %collective-permute-done.2.refs_8_ = bf16[4,64,512]{2,1,0:T(8,128)(2,1)S(1)} collective-permute-done((bf16[4,64,512]{2,1,0:T(8,128)(2,1)S(1)}, bf16[4,64,512]{2,1,0:T(8,128)(2,1)S(1)}, u32[]{:S(2)}, u32[]{:S(2)}) %collective-permute-start.2) | collective-permute-done | bytes 262176 | tf_op jit(solution)/shard_map/ppermute | solution.py:466
  26.5 3.9 %shard_map.85 = (f32[4,64,512]{2,1,0:T(8,128)S(1)}, bf16[4,64,512]{2,1,0:T(8,128)(2,1)S(1)}, bf16[4,64,512]{2,1,0:T(8,128)(2,1)S(1)}) custom-call(bf16[4,4,10,64,256]{4,3,2,1,0:T(8,128)(2,1)S(1)} %get-tuple-element.19.refs_0_, f32[4,2,8,64,256]{4,3,2,1,0:T(8,128)S(1)} %get-tuple-element.20.refs_1_, ...), custom_call_target="tpu_custom_call" | custom-call | flops 2952790016 | bytes 18270208 | tf_op jit(solution)/shard_map/pallas_call | solution.py:26
  30.4 0.7 %collective-permute-start.4 = (bf16[2,1,64,512]{3,2,1,0:T(8,128)(2,1)S(1)}, bf16[2,1,64,512]{3,2,1,0:T(8,128)(2,1)S(1)}, u32[]{:S(2)}, u32[]{:S(2)}) collective-permute-start(bf16[2,1,64,512]{3,2,1,0:T(8,128)(2,1)S(1)} %get-tuple-element.27), channel_id=1, source_target_pairs={{0,0},{1,2},{2,1},{3,4},{4,3},{5,6},{6,5},{7,7},{8,8},{9,10},{10,9... | collective-permute-start | bytes 393224 | tf_op jit(solution)/shard_map/ppermute | solution.py:405
  31.1 3.5 %collective-permute-start.3 = (bf16[2,1,64,512]{3,2,1,0:T(8,128)(2,1)S(1)}, bf16[2,1,64,512]{3,2,1,0:T(8,128)(2,1)S(1)}, u32[]{:S(2)}, u32[]{:S(2)}) collective-permute-start(bf16[2,1,64,512]{3,2,1,0:T(8,128)(2,1)S(1)} %get-tuple-element.28), channel_id=1, source_target_pairs={{0,1},{1,0},{2,3},{3,2},{4,5},{5,4},{6,7},{7,6},{8,9},{9,8},{10,11... | collective-permute-start | bytes 393224 | tf_op jit(solution)/shard_map/ppermute | solution.py:404
  34.6 0.0 slice-done
  34.6 0.0 slice-done.1
  34.6 0.0 slice-done.2
  34.6 0.0 slice-done.3
  34.6 2.1 %shard_map.87 = bf16[2,2,64,512]{3,2,1,0:T(8,128)(2,1)S(1)} custom-call(bf16[4,64,512]{2,1,0:T(8,128)(2,1)S(1)} %get-tuple-element.22.refs_0_.before_ref, bf16[4,64,512]{2,1,0:T(8,128)(2,1)S(1)} %get-tuple-element.23.refs_1_.latest_ref, bf16[3,3,3,512,512]{4,3,2,1,0:T(8,128)(2,1)S(1)} %bitcast.11), custom_call_target="tpu_custom_call" | custom-call | flops 1811939328 | bytes 14680064 | tf_op jit(solution)/shard_map/pallas_call | solution.py:26
  36.7 0.1 collective-permute-start.5
  36.8 0.0 collective-permute-done.4.refs_5_.far_ref
  36.8 0.0 collective-permute-done.3.refs_4_.near_ref
  36.8 2.1 %shard_map.88 = bf16[2,2,64,512]{3,2,1,0:T(8,128)(2,1)S(1)} custom-call(bf16[4,64,512]{2,1,0:T(8,128)(2,1)S(1)} %get-tuple-element.22.refs_0_.before_ref, bf16[4,64,512]{2,1,0:T(8,128)(2,1)S(1)} %get-tuple-element.23.refs_1_.latest_ref, bf16[2,1,64,512]{3,2,1,0:T(8,128)(2,1)S(1)} %collective-permute-done.3.refs_4_.near_ref, ...), custom_call_target="tpu_custom_call" | custom-call | flops 1811939328 | bytes 14942208 | tf_op jit(solution)/shard_map/pallas_call | solution.py:26
  38.9 3.5 %collective-permute-start.6 = (bf16[2,2,64,512]{3,2,1,0:T(8,128)(2,1)S(1)}, bf16[2,2,64,512]{3,2,1,0:T(8,128)(2,1)S(1)}, u32[]{:S(2)}, u32[]{:S(2)}) collective-permute-start(bf16[2,2,64,512]{3,2,1,0:T(8,128)(2,1)S(1)} %shard_map.88), channel_id=1, source_target_pairs={{0,8},{8,16},{16,24},{1,9},{9,17},{17,25},{2,10},{10,18},{18,26},{... | collective-permute-start | bytes 786440 | tf_op jit(solution)/shard_map/ppermute | solution.py:506
  42.4 4.1 %shard_map.86.own_ref = f32[2,4,64,512]{3,2,1,0:T(8,128)S(1)} custom-call(bf16[4,64,512]{2,1,0:T(8,128)(2,1)S(1)} %get-tuple-element.22.refs_0_.before_ref, bf16[4,64,512]{2,1,0:T(8,128)(2,1)S(1)} %get-tuple-element.23.refs_1_.latest_ref, f32[4,64,512]{2,1,0:T(8,128)S(1)} %get-tuple-element.24.refs_2_, f32[4,64,512]{2,1,0:T(8,128)S(1)} %shard_map.84.refs_9_.refs_3_, ...), custom_call_target="tpu_custom_call" | custom-call | flops 3623878656 | bytes 15990784 | tf_op jit(solution)/shard_map/pallas_call | solution.py:26
  46.5 0.3 collective-permute-done.5.inner_ref
  46.8 1.6 %collective-permute-done.6.outer_ref = bf16[2,2,64,512]{3,2,1,0:T(8,128)(2,1)S(1)} collective-permute-done((bf16[2,2,64,512]{3,2,1,0:T(8,128)(2,1)S(1)}, bf16[2,2,64,512]{3,2,1,0:T(8,128)(2,1)S(1)}, u32[]{:S(2)}, u32[]{:S(2)}) %collective-permute-start.6) | collective-permute-done | bytes 262176 | tf_op jit(solution)/shard_map/ppermute | solution.py:506
  48.4 0.9 %shard_map.89 = bf16[2,4,64,512]{3,2,1,0:T(8,128)(2,1)} custom-call(f32[2,4,64,512]{3,2,1,0:T(8,128)S(1)} %shard_map.86.own_ref, bf16[2,2,64,512]{3,2,1,0:T(8,128)(2,1)S(1)} %collective-permute-done.5.inner_ref, bf16[2,2,64,512]{3,2,1,0:T(8,128)(2,1)S(1)} %collective-permute-done.6.outer_ref), custom_call_target="tpu_custom_call" | custom-call | bytes 1572864 | tf_op jit(solution)/shard_map/pallas_call | solution.py:26
  (3 shorter events, 0.1 us)
Async XLA Ops:
  1.1 11.4 %collective-permute-start.1 = (bf16[4,1,128,256]{3,2,1,0:T(8,128)(2,1)S(1)}, bf16[4,1,128,256]{3,2,1,0:T(8,128)(2,1)S(1)}, u32[]{:S(2)}, u32[]{:S(2)}) collective-permute-start(bf16[4,1,128,256]{3,2,1,0:T(8,128)(2,1)S(1)} %get-tuple-element.25), channel_id=1, source_target_pairs={{0,0},{1,2},{2,1},{3,4},{4,3},{5,6},{6,5},{7,7},{8,8},{9,10},{10,9... | collective-permute-start | bytes 786440 | tf_op jit(solution)/shard_map/ppermute | solution.py:405
  1.8 10.8 %collective-permute-start = (bf16[4,1,128,256]{3,2,1,0:T(8,128)(2,1)S(1)}, bf16[4,1,128,256]{3,2,1,0:T(8,128)(2,1)S(1)}, u32[]{:S(2)}, u32[]{:S(2)}) collective-permute-start(bf16[4,1,128,256]{3,2,1,0:T(8,128)(2,1)S(1)} %get-tuple-element.26), channel_id=1, source_target_pairs={{0,1},{1,0},{2,3},{3,2},{4,5},{5,4},{6,7},{7,6},{8,9},{9,8},{10,11... | collective-permute-start | bytes 786440 | tf_op jit(solution)/shard_map/ppermute | solution.py:404
  6.1 6.4 %copy-start.3 = (f32[256]{0:T(256)S(1)}, f32[256]{0:T(256)}, u32[]{:S(2)}) copy-start(f32[256]{0:T(256)} %param.9) | copy-start | bytes 3076
  12.5 5.4 %copy-start = (bf16[2,24,4,64]{3,2,1,0:T(4,128)(2,1)S(1)}, bf16[2,24,4,64]{3,2,1,0:T(4,128)(2,1)}, u32[]{:S(2)}) copy-start(bf16[2,24,4,64]{3,2,1,0:T(4,128)(2,1)} %refs_5_.3) | copy-start | bytes 73732
  12.5 5.4 %copy-start.1 = (bf16[24,512]{1,0:T(8,128)(2,1)S(1)}, bf16[24,512]{1,0:T(8,128)(2,1)}, u32[]{:S(2)}) copy-start(bf16[24,512]{1,0:T(8,128)(2,1)} %refs_6_.4) | copy-start | bytes 73732
  12.6 5.4 %copy-start.2 = (f32[512]{0:T(512)S(1)}, f32[512]{0:T(512)}, u32[]{:S(2)}) copy-start(f32[512]{0:T(512)} %param.14) | copy-start | bytes 6148
  16.2 10.3 %collective-permute-start.2 = (bf16[4,64,512]{2,1,0:T(8,128)(2,1)S(1)}, bf16[4,64,512]{2,1,0:T(8,128)(2,1)S(1)}, u32[]{:S(2)}, u32[]{:S(2)}) collective-permute-start(bf16[4,64,512]{2,1,0:T(8,128)(2,1)S(1)} %get-tuple-element.21), channel_id=1, source_target_pairs={{0,8},{8,16},{16,24},{24,0},{1,9},{9,17},{17,25},{25,1},{2,10},{10... | collective-permute-start | bytes 786440 | tf_op jit(solution)/shard_map/ppermute | solution.py:466
  18.0 16.6 %slice-start = ((s8[14155776]{0:T(1024)(128)(4,1)}), s8[4194304]{0:T(1024)(128)(4,1)S(1)}, s32[]{:S(2)}) async-start(s8[14155776]{0:T(1024)(128)(4,1)} %bitcast.10), calls=%async_computation | async-start | bytes 8388608
  18.0 16.6 %slice-start.1 = ((s8[14155776]{0:T(1024)(128)(4,1)}), s8[4194304]{0:T(1024)(128)(4,1)S(1)}, s32[]{:S(2)}) async-start(s8[14155776]{0:T(1024)(128)(4,1)} %bitcast.10), calls=%async_computation.1 | async-start | bytes 8388608
  18.0 16.6 %slice-start.2 = ((s8[14155776]{0:T(1024)(128)(4,1)}), s8[4194304]{0:T(1024)(128)(4,1)S(1)}, s32[]{:S(2)}) async-start(s8[14155776]{0:T(1024)(128)(4,1)} %bitcast.10), calls=%async_computation.2 | async-start | bytes 8388608
  24.1 10.6 %slice-start.3 = ((s8[14155776]{0:T(1024)(128)(4,1)}), s8[1572864]{0:T(1024)(128)(4,1)S(1)}, s32[]{:S(2)}) async-start(s8[14155776]{0:T(1024)(128)(4,1)} %bitcast.10), calls=%async_computation.3 | async-start | bytes 3145728
  30.4 6.3 %collective-permute-start.4 = (bf16[2,1,64,512]{3,2,1,0:T(8,128)(2,1)S(1)}, bf16[2,1,64,512]{3,2,1,0:T(8,128)(2,1)S(1)}, u32[]{:S(2)}, u32[]{:S(2)}) collective-permute-start(bf16[2,1,64,512]{3,2,1,0:T(8,128)(2,1)S(1)} %get-tuple-element.27), channel_id=1, source_target_pairs={{0,0},{1,2},{2,1},{3,4},{4,3},{5,6},{6,5},{7,7},{8,8},{9,10},{10,9... | collective-permute-start | bytes 393224 | tf_op jit(solution)/shard_map/ppermute | solution.py:405
  31.1 5.7 %collective-permute-start.3 = (bf16[2,1,64,512]{3,2,1,0:T(8,128)(2,1)S(1)}, bf16[2,1,64,512]{3,2,1,0:T(8,128)(2,1)S(1)}, u32[]{:S(2)}, u32[]{:S(2)}) collective-permute-start(bf16[2,1,64,512]{3,2,1,0:T(8,128)(2,1)S(1)} %get-tuple-element.28), channel_id=1, source_target_pairs={{0,1},{1,0},{2,3},{3,2},{4,5},{5,4},{6,7},{7,6},{8,9},{9,8},{10,11... | collective-permute-start | bytes 393224 | tf_op jit(solution)/shard_map/ppermute | solution.py:404
  36.7 10.1 %collective-permute-start.5 = (bf16[2,2,64,512]{3,2,1,0:T(8,128)(2,1)S(1)}, bf16[2,2,64,512]{3,2,1,0:T(8,128)(2,1)S(1)}, u32[]{:S(2)}, u32[]{:S(2)}) collective-permute-start(bf16[2,2,64,512]{3,2,1,0:T(8,128)(2,1)S(1)} %shard_map.87), channel_id=1, source_target_pairs={{0,8},{8,16},{16,24},{24,0},{1,9},{9,17},{17,25},{25,1},{2,10},{10... | collective-permute-start | bytes 786440 | tf_op jit(solution)/shard_map/ppermute | solution.py:498
  38.9 9.6 %collective-permute-start.6 = (bf16[2,2,64,512]{3,2,1,0:T(8,128)(2,1)S(1)}, bf16[2,2,64,512]{3,2,1,0:T(8,128)(2,1)S(1)}, u32[]{:S(2)}, u32[]{:S(2)}) collective-permute-start(bf16[2,2,64,512]{3,2,1,0:T(8,128)(2,1)S(1)} %shard_map.88), channel_id=1, source_target_pairs={{0,8},{8,16},{16,24},{1,9},{9,17},{17,25},{2,10},{10,18},{18,26},{... | collective-permute-start | bytes 786440 | tf_op jit(solution)/shard_map/ppermute | solution.py:506
where the time goes:
time: 49.5 us; the launch traced here: 49.3 us
  Pallas kernels  29 us (59%)
  starting transfers between devices  14.6 us (29%)
  waiting for transfers between devices  4.39 us (9%)
  other arithmetic  1.1 us (2%)
    pallas_call x8, Pallas kernels, call(): pl.pallas_call(kernel, out_shape=outs, in_specs=[pl.BlockSpec(memory_spac...  29 us
    ppermute x2, starting transfers between devices, exchange(): lax.ppermute(jnp.where(odd, first_rows, last_rows), 'rows', routes[0])  7.87 us
    ppermute x1, starting transfers between devices, on_device(): outer = lax.ppermute(outer, 'tm', chain('tm', WRAPS[2]))  3.53 us
    ppermute x1, waiting for transfers between devices, on_device(): carried = lax.ppermute(carry, 'tm', chain('tm', WRAPS[0]))  2.43 us
    ppermute x1, starting transfers between devices, on_device(): carried = lax.ppermute(carry, 'tm', chain('tm', WRAPS[0]))  1.81 us
    ppermute x1, waiting for transfers between devices, on_device(): outer = lax.ppermute(outer, 'tm', chain('tm', WRAPS[2]))  1.62 us
    ppermute x2, starting transfers between devices, exchange(): far = lax.ppermute(jnp.where(odd, last_rows, first_rows), 'rows', routes[1])  1.35 us
    select_n x2, other arithmetic, exchange(): far = lax.ppermute(jnp.where(odd, last_rows, first_rows), 'rows', routes[1])  1.1 us
  transfers between devices with their start and end apart: 7, of which 3 were waited for; matrix products, arithmetic and copies ran while one was open for 0% of the time, Pallas kernels for 42%

commit v1 on v0

--- a/solution.py
+++ b/solution.py
@@ -79,31 +79,41 @@
     pad_ref[1, :, ext - PAD :, :] = zero
 
 
+def rows_kernel(feat_hbm, gain_hbm, near_ref, far_ref, start_ref, gain_ref, sem):
+    height = feat_hbm.shape[1]
+    odd = lax.rem(lax.axis_index("rows"), 2)
+    pairs = [
+        (feat_hbm.at[:, pl.ds((height - 1) * use_last, 1)], ref)
+        for ref, use_last in ((far_ref, odd), (near_ref, 1 - odd))
+    ] + [(gain_hbm, gain_ref), (feat_hbm.at[0:1], start_ref)]
+    copies = [pltpu.make_async_copy(src, dst, sem.at[n]) for n, (src, dst) in enumerate(pairs)]
+    for copy in copies:
+        copy.start()
+    for copy in copies:
+        copy.wait()
+
+
 def norm_kernel(
-    feat_hbm, gain_hbm, down_hbm, w_hbm, x_ref, res_ref, v_ref, g_ref, w_ref,
-    feat_ref, gain_ref, down_ref, raw_ref, pad_ref, feat_sem, gain_sem, down_sem, w_sem,
-    *, step
+    start_ref, gain_ref, feat_hbm, down_hbm, w_hbm, x_ref, res_ref, v_ref, g_ref, w_ref, lev_ref,
+    own_lev_ref, feat_ref, down_ref, raw_ref, pad_ref, feat_sem, down_sem, w_sem, *, step
 ):
-    frames, height, _, channels = feat_ref.shape
+    _, height, _, channels = start_ref.shape
+    frames = x_ref.shape[0]
     feat_copies = [
-        pltpu.make_async_copy(feat_hbm.at[f], feat_ref.at[f], feat_sem.at[f])
-        for f in range(frames)
+        pltpu.make_async_copy(feat_hbm.at[f], feat_ref.at[f - 1], feat_sem.at[f - 1])
+        for f in range(1, frames)
     ]
     w_copies = [pltpu.make_async_copy(w_hbm.at[a], w_ref.at[a], w_sem.at[a]) for a in range(3)]
     down_copy = pltpu.make_async_copy(down_hbm, down_ref, down_sem)
-    gain_copy = pltpu.make_async_copy(gain_hbm, gain_ref, gain_sem)
-    later_copies = [*w_copies, down_copy]
-    for copy in (gain_copy, *feat_copies):
+    for copy in (*feat_copies, *w_copies, down_copy):
         copy.start()
     clear_pads(pad_ref)
-    gain_copy.wait()
     gain = gain_ref[...]
 
     for f in range(frames):
-        feat_copies[f].wait()
-        if f == 0:
-            for copy in later_copies:
-                copy.start()
+        frame_ref = start_ref.at[0] if f == 0 else feat_ref.at[f - 1]
+        if f > 0:
+            feat_copies[f - 1].wait()
 
         def body(index, carry):
             h = index * step
@@ -114,7 +124,7 @@
             def residual(r, value):
                 res_ref[f, r, pl.ds(h, step)] = value
 
-            prepare(feat_ref[f, pl.ds(h, step)], gain, raw_ref, pad_ref, store, residual)
+            prepare(frame_ref[pl.ds(h, step)], gain, raw_ref, pad_ref, store, residual)
             return carry
 
         lax.fori_loop(0, height // step, body, 0)
@@ -147,53 +157,66 @@
         return carry
 
     lax.fori_loop(0, channels // rows, fold, 0)
-
-
-def conv_pair(pair, x_ref, w_ref, g_ref, res_ref, v_ref, lev_ref, group):
-    frames, _, ext, half, channels = x_ref.shape
-    deep_rows = (ext - 2) // 2
-
-    for index in range(deep_rows // group):
-        start = 2 * group * index
-        for i in range(2):
-            f = 2 * pair + i
-            taps = [a for a in range(3) if 0 <= f + a - 2 < frames]
-            sums = []
-            for t in range(4):
-                total = None
-                for a in taps:
-                    for b in range(3):
-                        rows = x_ref[f + a - 2, t, pl.ds(start + b, 2 * group)].reshape(
-                            2 * group * half, channels
-                        )
-                        weight = (
-                            w_ref[a, b, 0], g_ref[a, b, 0], g_ref[a, b, 1], w_ref[a, b, 2]
-                        )[t]
-                        part = jnp.dot(rows, weight, preferred_element_type=jnp.float32)
-                        total = part if total is None else total + part
-                sums.append(total)
-            pieces = (sums[0] - sums[3] + sums[1], sums[0] + sums[3] + sums[2])
-            for r in range(2):
-                level = pieces[r].reshape(2 * group, half, channels)
-                if res_ref is not None:
-                    level = level + res_ref[f, r, pl.ds(start, 2 * group)]
-                level = level.astype(jnp.bfloat16)
-                for row in range(2 * group):
-                    lev_ref[4 * i + 2 * (row % 2) + r, index * group + row // 2] = level[row]
+    inner, _ = groups_of(height // 2)
+    for deep_rows in inner:
+        conv_rows(frames // 2, deep_rows, x_ref, w_ref, g_ref, None, lev_ref)
+        conv_rows(frames // 2 - 1, deep_rows, x_ref, w_ref, g_ref, res_ref, own_lev_ref, (0,))
+
+
+def groups_of(deep_rows):
+    inner = range(1, deep_rows - 1)
+    return [tuple(inner[n : n + 2]) for n in range(0, len(inner), 2)], (0, deep_rows - 1)
+
+
+def conv_rows(pair, deep_rows, x_ref, w_ref, g_ref, res_ref, lev_ref, parts=(0, 1)):
+    frames, _, _, half, channels = x_ref.shape
+    for i in parts:
+        f = 2 * pair + i
+        taps = [a for a in range(3) if 0 <= f + a - 2 < frames]
+        sums = []
+        for t in range(4):
+            total = None
+            for a in taps:
+                for b in range(3):
+                    rows = jnp.concatenate(
+                        [
+                            x_ref[f + a - 2, t, 2 * h + b : 2 * h + b + 2].reshape(
+                                2 * half, channels
+                            )
+                            for h in deep_rows
+                        ],
+                        0,
+                    )
+                    weight = (w_ref[a, b, 0], g_ref[a, b, 0], g_ref[a, b, 1], w_ref[a, b, 2])[t]
+                    part = dot(rows, weight)
+                    total = part if total is None else total + part
+            sums.append(total)
+        pieces = (sums[0] - sums[3] + sums[1], sums[0] + sums[3] + sums[2])
+        for r in range(2):
+            for n, h in enumerate(deep_rows):
+                for j in range(2):
+                    at = (2 * n + j) * half
+                    level = pieces[r][at : at + half]
+                    if res_ref is not None:
+                        level = level + res_ref[f, r, 2 * h + j]
+                    lev_ref[4 * i + 2 * j + r, h] = level.astype(jnp.bfloat16)
+
+
+def project(lev_ref, v_ref):
     total = None
     for s in range(8):
-        part = jnp.dot(
-            lev_ref[s].reshape(deep_rows * half, channels),
-            v_ref[s],
-            preferred_element_type=jnp.float32,
-        )
+        part = dot(lev_ref[s].reshape(-1, lev_ref.shape[-1]), v_ref[s])
         total = part if total is None else total + part
     return total * haar_scale
 
 
+def dot(rows, weight):
+    return jnp.dot(rows, weight, preferred_element_type=jnp.float32)
+
+
 def carry_kernel(
-    x_in, near_ref, far_ref, gain_ref, w_ref, g_ref, v_ref, x_ref, out_ref,
-    lev_ref, raw_ref, pad_ref, *, group
+    x_in, lev_in, near_ref, far_ref, gain_ref, w_ref, g_ref, v_ref, x_ref, lev_ref, out_ref,
+    raw_ref, pad_ref
 ):
     frames, _, ext, _, _ = x_ref.shape
     gain = gain_ref[...]
@@ -213,37 +236,46 @@
             )
 
     halos(frames - 2, 2)
-    projected = conv_pair(frames // 2, x_ref, w_ref, g_ref, None, v_ref, lev_ref, group)
+    _, outer = groups_of((ext - 2) // 2)
+    conv_rows(frames // 2, outer, x_ref, w_ref, g_ref, None, lev_ref)
+    projected = project(lev_ref, v_ref)
     out_ref[...] = projected.reshape(out_ref.shape).astype(out_ref.dtype)
     halos(0, frames - 2)
 
 
-def own_kernel(*refs, pair, extra, group, later):
-    x_ref, res_ref, w_ref, g_ref, v_ref, wav_ref, inj_ref, gain_ref = refs[:8]
-    carried_ref = refs[8] if extra else None
-    later_refs = refs[8 + extra : 8 + extra + later]
-    outs = refs[8 + extra + later :]
-    deep_ref, lev_ref = outs[0], outs[-1]
-    normed_refs = outs[1:-1]
+def own_kernel(lev_in, x_ref, res_ref, w_ref, g_ref, v_ref, wav_ref, inj_ref, gain_ref, *outs):
+    last_lev_ref, lev_ref = outs[0], outs[-1]
+    deep_frames = wav_ref.shape[0]
+    deep_refs, normed_refs = outs[1 : 1 + deep_frames], outs[1 + deep_frames : -1]
     gain = gain_ref[...]
-    injected = [
-        lax.dot_general(
-            wav_ref[pair, :, h, :],
-            inj_ref[...],
-            (((0,), (0,)), ((), ())),
-            preferred_element_type=jnp.float32,
-        )
-        for h in range(wav_ref.shape[2])
-    ]
-    for ref, out in zip(later_refs, normed_refs[1:]):
-        out[...] = norm_act(ref[...], gain).astype(out.dtype)
-    value = conv_pair(pair, x_ref, w_ref, g_ref, res_ref, v_ref, lev_ref, group)
-    value = value + jnp.concatenate(injected, 0)
-    if extra:
-        value = value + arrived(carried_ref[...].reshape(value.shape))
-    deep_ref[...] = value.reshape(deep_ref.shape)
-    if extra:
-        normed_refs[0][...] = norm_act(value, gain).reshape(deep_ref.shape).astype(jnp.bfloat16)
+    inner, outer = groups_of(lev_ref.shape[2])
+    for pair in reversed(range(deep_frames)):
+        last = pair == deep_frames - 1
+        level = last_lev_ref if last else lev_ref.at[pair % 2]
+        for deep_rows in inner:
+            parts = (1,) if last else (0, 1)
+            conv_rows(pair, deep_rows, x_ref, w_ref, g_ref, res_ref, level, parts)
+        conv_rows(pair, outer, x_ref, w_ref, g_ref, res_ref, level)
+        injected = [
+            lax.dot_general(
+                wav_ref[pair, :, h, :],
+                inj_ref[...],
+                (((0,), (0,)), ((), ())),
+                preferred_element_type=jnp.float32,
+            )
+            for h in range(wav_ref.shape[2])
+        ]
+        value = project(level, v_ref) + jnp.concatenate(injected, 0)
+        deep_refs[pair][...] = value.reshape(deep_refs[pair].shape)
+        if pair > 0:
+            out = normed_refs[pair - 1]
+            out[...] = norm_act(value, gain).reshape(out.shape).astype(out.dtype)
+
+
+def first_kernel(partial_ref, carried_ref, gain_ref, deep_ref, normed_ref):
+    value = partial_ref[...] + arrived(carried_ref[...])
+    deep_ref[...] = value
+    normed_ref[...] = norm_act(value, gain_ref[...]).astype(normed_ref.dtype)
 
 
 def shifted(z_ref, sums):
@@ -263,10 +295,6 @@
     zero = jnp.zeros((rows, PAD, channels), jnp.float32)
     z_ref[0, :, 0:PAD, :] = zero
     z_ref[2, :, ext - PAD :, :] = zero
-
-
-def dot(rows, weight):
-    return jnp.dot(rows, weight, preferred_element_type=jnp.float32)
 
 
 def deep_conv(targets, ext_ref, w_ref, z_ref):
@@ -398,11 +426,10 @@
     return above, jnp.where(index == count - 1, jnp.zeros_like(below), below)
 
 
-def exchange(first_rows, last_rows):
-    odd = lax.rem(lax.axis_index("rows"), 2) == 1
+def exchange(near, far):
     routes = neighbours("rows")
-    near = lax.ppermute(jnp.where(odd, first_rows, last_rows), "rows", routes[0])
-    far = lax.ppermute(jnp.where(odd, last_rows, first_rows), "rows", routes[1])
+    near = lax.ppermute(near, "rows", routes[0])
+    far = lax.ppermute(far, "rows", routes[1])
     return near, far
 
 
@@ -412,18 +439,31 @@
     frames, height, width, channels = feat_mid.shape
     deep_channels = down_weight.shape[-1]
     deep_frames, deep_rows, half = frames // 2, height // 2, width // 2
-    group = 2 if deep_rows % 2 == 0 else 1
     bf16, f32 = jnp.bfloat16, jnp.float32
     shape = jax.ShapeDtypeStruct
     local = pltpu.VMEM
     gain_mid = gain_mid.reshape(1, -1)
     gain_deep = gain_deep.reshape(1, -1)
 
-    near, far = exchange(feat_mid[:, :1], feat_mid[:, height - 1 :])
+    rows_shape = shape((frames, 1, width, channels), bf16)
+    near, far, start, gain_mid = call(
+        rows_kernel,
+        (
+            rows_shape,
+            rows_shape,
+            local((1, height, width, channels), bf16),
+            local(gain_mid.shape, f32),
+        ),
+        (feat_mid, gain_mid),
+        (pltpu.SemaphoreType.DMA((4,)),),
+        hbm=(0, 1),
+    )
+    near, far = exchange(near, far)
     x_shape = local((frames, 4, height + 2, half, channels), bf16)
     step = 4
+    lev_shape = local((8, deep_rows, half, channels), bf16)
     sem = pltpu.SemaphoreType.DMA
-    x, residual, folded, mixed, conv_mid = call(
+    x, residual, folded, mixed, conv_mid, levels, own_levels = call(
         functools.partial(norm_kernel, step=step),
         (
             x_shape,
@@ -431,58 +471,60 @@
             local(down_weight.shape, bf16),
             local((3, 3, 2) + conv_mid.shape[-2:], bf16),
             local(conv_mid.shape, bf16),
+            lev_shape,
+            lev_shape,
         ),
-        (feat_mid, gain_mid, down_weight, conv_mid),
+        (start, gain_mid, feat_mid, down_weight, conv_mid),
         (
-            pltpu.VMEM(feat_mid.shape, bf16),
-            pltpu.VMEM(gain_mid.shape, f32),
+            pltpu.VMEM((frames - 1, height, width, channels), bf16),
             pltpu.VMEM(down_weight.shape, bf16),
             pltpu.VMEM((step, channels // 128, width, 128), f32),
             pltpu.VMEM((2, step, half + 2 * PAD, channels), f32),
-            sem((frames,)),
-            sem(()),
+            sem((frames - 1,)),
             sem(()),
             sem((3,)),
         ),
         flops=5e9,
-        hbm=(0, 1, 2, 3),
-    )
-    lev = pltpu.VMEM((8, deep_rows, half, channels), bf16)
+        hbm=(2, 3, 4),
+    )
     tap = 2 * height * width * channels * channels * 6
     proj = 2 * deep_rows * half * 8 * channels * deep_channels
 
-    x, carry = call(
-        functools.partial(carry_kernel, group=group),
-        (x_shape, shape((deep_rows, half, deep_channels), bf16)),
-        (x, near, far, gain_mid, conv_mid, mixed, folded),
+    x, levels, carry = call(
+        carry_kernel,
+        (x_shape, lev_shape, shape((deep_rows, half, deep_channels), bf16)),
+        (x, levels, near, far, gain_mid, conv_mid, mixed, folded),
         (
-            lev,
             pltpu.VMEM((frames, channels // 128, width, 128), f32),
             pltpu.VMEM((2, frames, half + 2 * PAD, channels), f32),
         ),
         flops=3 * tap + proj,
+        aliases={0: 0, 1: 1},
+    )
+    carried = lax.ppermute(carry, "tm", chain("tm", WRAPS[0]))
+    deep_shape = (deep_rows, half, deep_channels)
+    _, *made = call(
+        own_kernel,
+        (lev_shape,)
+        + (shape(deep_shape, f32),) * deep_frames
+        + (shape(deep_shape, bf16),) * (deep_frames - 1),
+        (own_levels, x, residual, conv_mid, mixed, folded, wavelets, inject_weight, gain_deep),
+        (pltpu.VMEM((2, 8, deep_rows, half, channels), bf16),),
+        flops=deep_frames * (6 * tap + proj) - 3 * tap,
         aliases={0: 0},
     )
-    carried = lax.ppermute(carry, "tm", chain("tm", WRAPS[0]))
-    deep = [None] * deep_frames
-    for pair in reversed(range(deep_frames)):
-        extra = pair == 0
-        later = tuple(deep[1:]) if extra else ()
-        made = call(
-            functools.partial(own_kernel, pair=pair, extra=extra, group=group, later=len(later)),
-            (shape((deep_rows, half, deep_channels), f32),)
-            + (shape((deep_rows, half, deep_channels), bf16),) * (extra * deep_frames),
-            (x, residual, conv_mid, mixed, folded, wavelets, inject_weight, gain_deep)
-            + ((carried,) if extra else ())
-            + later,
-            (lev,),
-            flops=(3 if extra else 6) * tap + proj,
-        )
-        deep[pair] = made[0]
-    normed = made[1:]
-    near, far = exchange(
-        jnp.stack([n[:1] for n in normed]), jnp.stack([n[deep_rows - 1 :] for n in normed])
-    )
+    partial, *deep = made[:deep_frames]
+    first, normed = call(
+        first_kernel,
+        (shape(deep_shape, f32), shape(deep_shape, bf16)),
+        (partial, carried, gain_deep),
+        flops=1e8,
+    )
+    deep, normed = [first, *deep], [normed, *made[deep_frames:]]
+    odd = lax.rem(lax.axis_index("rows"), 2) == 1
+    first = jnp.stack([n[:1] for n in normed])
+    last = jnp.stack([n[deep_rows - 1 :] for n in normed])
+    near, far = exchange(jnp.where(odd, first, last), jnp.where(odd, last, first))
     ext = pltpu.VMEM((deep_frames, deep_rows + 2, half, deep_channels), bf16)
     z = pltpu.VMEM((3, deep_rows, half + 2 * PAD, deep_channels), f32)
     tap = 2 * deep_rows * half * deep_channels * deep_channels * 9

time: 49.5 us -> 46 us (0.929)
  the two profiles are of different devices: /device:TPU:0 before, /device:TPU:20 now
where the time goes in v1:
time: 46 us; the launch traced here: 45.8 us
  Pallas kernels  29.1 us (63%)
  starting transfers between devices  11.4 us (25%)
  waiting for transfers between devices  4.93 us (11%)
    pallas_call x9, Pallas kernels, call(): pl.pallas_call(kernel, out_shape=outs, in_specs=[pl.BlockSpec(memory_spac...  29.1 us
    ppermute x2, starting transfers between devices, exchange(): far = lax.ppermute(far, 'rows', routes[1])  6.17 us
    ppermute x1, waiting for transfers between devices, on_device(): outer = lax.ppermute(outer, 'tm', chain('tm', WRAPS[2]))  3.03 us
    ppermute x1, starting transfers between devices, on_device(): outer = lax.ppermute(outer, 'tm', chain('tm', WRAPS[2]))  2.45 us
    ppermute x2, waiting for transfers between devices, exchange(): far = lax.ppermute(far, 'rows', routes[1])  1.88 us
    ppermute x1, starting transfers between devices, on_device(): carried = lax.ppermute(carry, 'tm', chain('tm', WRAPS[0]))  1.83 us
  transfers between devices with their start and end apart: 7, of which 2 were waited for; matrix products, arithmetic and copies ran while one was open for 0% of the time, Pallas kernels for 53%

profile of v1, /device:TPU:20, one launch (start us, length us, event | category | flops | bytes accessed | tf_op | source)
XLA Modules:
  0.0 45.8 jit_solution(8552550879160933858)
XLA Ops:
  0.0 1.3 %shard_map.82 = (bf16[4,1,128,256]{3,2,1,0:T(8,128)(2,1)S(1)}, bf16[4,1,128,256]{3,2,1,0:T(8,128)(2,1)S(1)}, bf16[1,8,128,256]{3,2,1,0:T(8,128)(2,1)S(1)}, f32[1,256]{1,0:T(1,128)S(1)}) custom-call(bf16[4,8,128,256]{3,2,1,0:T(8,128)(2,1)} %feat_hbm.3, f32[1,256]{1,0:T(1,128)} %bitcast.14), custom_call_target="tpu_custom_call" | custom-call | bytes 2098176 | tf_op jit(solution)/shard_map/pallas_call | solution.py:26
  1.3 0.1 collective-permute-start
  1.3 3.4 %collective-permute-start.1 = (bf16[4,1,128,256]{3,2,1,0:T(8,128)(2,1)S(1)}, bf16[4,1,128,256]{3,2,1,0:T(8,128)(2,1)S(1)}, u32[]{:S(2)}, u32[]{:S(2)}) collective-permute-start(bf16[4,1,128,256]{3,2,1,0:T(8,128)(2,1)S(1)} %get-tuple-element.29), channel_id=1, source_target_pairs={{0,0},{1,2},{2,1},{3,4},{4,3},{5,6},{6,5},{7,7},{8,8},{9,10},{10,9... | collective-permute-start | bytes 786440 | tf_op jit(solution)/shard_map/ppermute | solution.py:432
  4.8 7.9 %shard_map.83 = (bf16[4,4,10,64,256]{4,3,2,1,0:T(8,128)(2,1)S(1)}, f32[4,2,8,64,256]{4,3,2,1,0:T(8,128)S(1)}, bf16[8,256,512]{2,1,0:T(8,128)(2,1)S(1)}, bf16[3,3...) custom-call(bf16[1,8,128,256]{3,2,1,0:T(8,128)(2,1)S(1)} %get-tuple-, ...), custom_call_target="tpu_custom_call" | custom-call | flops 5000000000 | bytes 8258560 | tf_op jit(solution)/shard_map/pallas_call | solution.py:26
  12.7 0.0 collective-permute-done.near_ref
  12.7 0.0 collective-permute-done.1.far_ref
  12.7 0.0 copy-start
  12.8 0.0 copy-start.1
  12.8 0.0 copy-start.2
  12.8 2.4 %shard_map.84 = (bf16[4,4,10,64,256]{4,3,2,1,0:T(8,128)(2,1)S(1)}, bf16[8,4,64,256]{3,2,1,0:T(8,128)(2,1)S(1)}, bf16[4,64,512]{2,1,0:T(8,128)(2,1)S(1)}) custom-call(bf16[4,4,10,64,256]{4,3,2,1,0:T(8,128)(2,1)S(1)} %get-tuple-element.26.x_in, bf16[8,4,64,256]{3,2,1,0:T(8,128)(2,1)S(1)} %get-tuple-element.27.lev_in, ...), custom_call_target="tpu_custom_call", output_to_operand_aliasing={{0}: (0, {}), {1}: (1, {})} | custom-call | flops 2952790016 | bytes 14812160 | tf_op jit(solution)/shard_map/pallas_call | solution.py:26
  15.2 1.8 %collective-permute-start.2 = (bf16[4,64,512]{2,1,0:T(8,128)(2,1)S(1)}, bf16[4,64,512]{2,1,0:T(8,128)(2,1)S(1)}, u32[]{:S(2)}, u32[]{:S(2)}) collective-permute-start(bf16[4,64,512]{2,1,0:T(8,128)(2,1)S(1)} %get-tuple-element.36), channel_id=1, source_target_pairs={{0,8},{8,16},{16,24},{24,0},{1,9},{9,17},{17,25},{25,1},{2,10},{10... | collective-permute-start | bytes 786440 | tf_op jit(solution)/shard_map/ppermute | solution.py:504
  17.0 0.0 slice-start
  17.0 0.0 copy-done
  17.0 0.0 copy-done.1
  17.0 0.0 copy-done.2
  17.0 0.0 slice-start.1
  17.0 0.0 slice-start.2
  17.0 0.0 slice-start.3
  17.1 8.1 %shard_map.85 = (bf16[8,4,64,256]{3,2,1,0:T(8,128)(2,1)S(1)}, f32[4,64,512]{2,1,0:T(8,128)S(1)}, f32[4,64,512]{2,1,0:T(8,128)S(1)}, bf16[4,64,512]{2,1,0:T(8,128)(2,1)S(1)}) custom-call(bf16[8,4,64,256]{3,2,1,0:T(8,128)(2,1)S(1)} %get-tuple-element.25.lev_in, ...), custom_call_target="tpu_custom_call", output_to_operand_aliasing={{0}: (0, {})} | custom-call | flops 8321499136 | bytes 18532352 | tf_op jit(solution)/shard_map/pallas_call | solution.py:26
  25.2 0.0 collective-permute-done.2.carried_ref
  25.2 0.3 shard_map.86
  25.5 0.1 collective-permute-start.3
  25.6 2.7 %collective-permute-start.4 = (bf16[2,1,64,512]{3,2,1,0:T(8,128)(2,1)S(1)}, bf16[2,1,64,512]{3,2,1,0:T(8,128)(2,1)S(1)}, u32[]{:S(2)}, u32[]{:S(2)}) collective-permute-start(bf16[2,1,64,512]{3,2,1,0:T(8,128)(2,1)S(1)} %get-tuple-element.41), channel_id=1, source_target_pairs={{0,0},{1,2},{2,1},{3,4},{4,3},{5,6},{6,5},{7,7},{8,8},{9,10},{10,9... | collective-permute-start | bytes 393224 | tf_op jit(solution)/shard_map/ppermute | solution.py:432
  28.4 0.0 slice-done
  28.4 0.0 slice-done.1
  28.4 0.0 slice-done.2
  28.4 0.0 slice-done.3
  28.4 2.1 %shard_map.88 = bf16[2,2,64,512]{3,2,1,0:T(8,128)(2,1)S(1)} custom-call(bf16[4,64,512]{2,1,0:T(8,128)(2,1)S(1)} %get-tuple-element.37.refs_0_.before_ref, bf16[4,64,512]{2,1,0:T(8,128)(2,1)S(1)} %get-tuple-element.38.refs_1_.latest_ref, bf16[3,3,3,512,512]{4,3,2,1,0:T(8,128)(2,1)S(1)} %bitcast.11), custom_call_target="tpu_custom_call" | custom-call | flops 1811939328 | bytes 14680064 | tf_op jit(solution)/shard_map/pallas_call | solution.py:26
  30.5 0.8 %collective-permute-start.5 = (bf16[2,2,64,512]{3,2,1,0:T(8,128)(2,1)S(1)}, bf16[2,2,64,512]{3,2,1,0:T(8,128)(2,1)S(1)}, u32[]{:S(2)}, u32[]{:S(2)}) collective-permute-start(bf16[2,2,64,512]{3,2,1,0:T(8,128)(2,1)S(1)} %shard_map.88), channel_id=1, source_target_pairs={{0,8},{8,16},{16,24},{24,0},{1,9},{9,17},{17,25},{25,1},{2,10},{10... | collective-permute-start | bytes 786440 | tf_op jit(solution)/shard_map/ppermute | solution.py:540
  31.3 0.0 collective-permute-done.3.refs_4_.near_ref
  31.3 1.9 %collective-permute-done.4.refs_5_.far_ref = bf16[2,1,64,512]{3,2,1,0:T(8,128)(2,1)S(1)} collective-permute-done((bf16[2,1,64,512]{3,2,1,0:T(8,128)(2,1)S(1)}, bf16[2,1,64,512]{3,2,1,0:T(8,128)(2,1)S(1)}, u32[]{:S(2)}, u32[]{:S(2)}) %collective-permute-start.4) | collective-permute-done | bytes 131104 | tf_op jit(solution)/shard_map/ppermute | solution.py:432
  33.2 2.1 %shard_map.89 = bf16[2,2,64,512]{3,2,1,0:T(8,128)(2,1)S(1)} custom-call(bf16[4,64,512]{2,1,0:T(8,128)(2,1)S(1)} %get-tuple-element.37.refs_0_.before_ref, bf16[4,64,512]{2,1,0:T(8,128)(2,1)S(1)} %get-tuple-element.38.refs_1_.latest_ref, bf16[2,1,64,512]{3,2,1,0:T(8,128)(2,1)S(1)} %collective-permute-done.3.refs_4_.near_ref, ...), custom_call_target="tpu_custom_call" | custom-call | flops 1811939328 | bytes 14942208 | tf_op jit(solution)/shard_map/pallas_call | solution.py:26
  35.3 2.4 %collective-permute-start.6 = (bf16[2,2,64,512]{3,2,1,0:T(8,128)(2,1)S(1)}, bf16[2,2,64,512]{3,2,1,0:T(8,128)(2,1)S(1)}, u32[]{:S(2)}, u32[]{:S(2)}) collective-permute-start(bf16[2,2,64,512]{3,2,1,0:T(8,128)(2,1)S(1)} %shard_map.89), channel_id=1, source_target_pairs={{0,8},{8,16},{16,24},{1,9},{9,17},{17,25},{2,10},{10,18},{18,26},{... | collective-permute-start | bytes 786440 | tf_op jit(solution)/shard_map/ppermute | solution.py:548
  37.8 4.1 %shard_map.87.own_ref = f32[2,4,64,512]{3,2,1,0:T(8,128)S(1)} custom-call(bf16[4,64,512]{2,1,0:T(8,128)(2,1)S(1)} %get-tuple-element.37.refs_0_.before_ref, bf16[4,64,512]{2,1,0:T(8,128)(2,1)S(1)} %get-tuple-element.38.refs_1_.latest_ref, f32[4,64,512]{2,1,0:T(8,128)S(1)} %get-tuple-element.39.refs_2_, f32[4,64,512]{2,1,0:T(8,128)S(1)} %get-tuple-element.40.refs_3_, ...), custom_call_target="tpu_custom_call" | custom-call | flops 3623878656 | bytes 15990784 | tf_op jit(solution)/shard_map/pallas_call | solution.py:26
  41.8 0.0 collective-permute-done.5.inner_ref
  41.8 3.0 %collective-permute-done.6.outer_ref = bf16[2,2,64,512]{3,2,1,0:T(8,128)(2,1)S(1)} collective-permute-done((bf16[2,2,64,512]{3,2,1,0:T(8,128)(2,1)S(1)}, bf16[2,2,64,512]{3,2,1,0:T(8,128)(2,1)S(1)}, u32[]{:S(2)}, u32[]{:S(2)}) %collective-permute-start.6) | collective-permute-done | bytes 262176 | tf_op jit(solution)/shard_map/ppermute | solution.py:548
  44.9 0.9 %shard_map.90 = bf16[2,4,64,512]{3,2,1,0:T(8,128)(2,1)} custom-call(f32[2,4,64,512]{3,2,1,0:T(8,128)S(1)} %shard_map.87.own_ref, bf16[2,2,64,512]{3,2,1,0:T(8,128)(2,1)S(1)} %collective-permute-done.5.inner_ref, bf16[2,2,64,512]{3,2,1,0:T(8,128)(2,1)S(1)} %collective-permute-done.6.outer_ref), custom_call_target="tpu_custom_call" | custom-call | bytes 1572864 | tf_op jit(solution)/shard_map/pallas_call | solution.py:26
  (3 shorter events, 0.1 us)
Async XLA Ops:
  1.3 11.5 %collective-permute-start = (bf16[4,1,128,256]{3,2,1,0:T(8,128)(2,1)S(1)}, bf16[4,1,128,256]{3,2,1,0:T(8,128)(2,1)S(1)}, u32[]{:S(2)}, u32[]{:S(2)}) collective-permute-start(bf16[4,1,128,256]{3,2,1,0:T(8,128)(2,1)S(1)} %get-tuple-element.28), channel_id=1, source_target_pairs={{0,1},{1,0},{2,3},{3,2},{4,5},{5,4},{6,7},{7,6},{8,9},{9,8},{10,11... | collective-permute-start | bytes 786440 | tf_op jit(solution)/shard_map/ppermute | solution.py:431
  1.3 11.4 %collective-permute-start.1 = (bf16[4,1,128,256]{3,2,1,0:T(8,128)(2,1)S(1)}, bf16[4,1,128,256]{3,2,1,0:T(8,128)(2,1)S(1)}, u32[]{:S(2)}, u32[]{:S(2)}) collective-permute-start(bf16[4,1,128,256]{3,2,1,0:T(8,128)(2,1)S(1)} %get-tuple-element.29), channel_id=1, source_target_pairs={{0,0},{1,2},{2,1},{3,4},{4,3},{5,6},{6,5},{7,7},{8,8},{9,10},{10,9... | collective-permute-start | bytes 786440 | tf_op jit(solution)/shard_map/ppermute | solution.py:432
  12.7 4.3 %copy-start = (f32[512]{0:T(512)S(1)}, f32[512]{0:T(512)}, u32[]{:S(2)}) copy-start(f32[512]{0:T(512)} %param.14) | copy-start | bytes 6148
  12.8 4.3 %copy-start.1 = (bf16[2,24,4,64]{3,2,1,0:T(4,128)(2,1)S(1)}, bf16[2,24,4,64]{3,2,1,0:T(4,128)(2,1)}, u32[]{:S(2)}) copy-start(bf16[2,24,4,64]{3,2,1,0:T(4,128)(2,1)} %wav_ref.1) | copy-start | bytes 73732
  12.8 4.2 %copy-start.2 = (bf16[24,512]{1,0:T(8,128)(2,1)S(1)}, bf16[24,512]{1,0:T(8,128)(2,1)}, u32[]{:S(2)}) copy-start(bf16[24,512]{1,0:T(8,128)(2,1)} %inj_ref.1) | copy-start | bytes 73732
  15.2 10.0 %collective-permute-start.2 = (bf16[4,64,512]{2,1,0:T(8,128)(2,1)S(1)}, bf16[4,64,512]{2,1,0:T(8,128)(2,1)S(1)}, u32[]{:S(2)}, u32[]{:S(2)}) collective-permute-start(bf16[4,64,512]{2,1,0:T(8,128)(2,1)S(1)} %get-tuple-element.36), channel_id=1, source_target_pairs={{0,8},{8,16},{16,24},{24,0},{1,9},{9,17},{17,25},{25,1},{2,10},{10... | collective-permute-start | bytes 786440 | tf_op jit(solution)/shard_map/ppermute | solution.py:504
  17.0 11.4 %slice-start = ((s8[14155776]{0:T(1024)(128)(4,1)}), s8[4194304]{0:T(1024)(128)(4,1)S(1)}, s32[]{:S(2)}) async-start(s8[14155776]{0:T(1024)(128)(4,1)} %bitcast.10), calls=%async_computation | async-start | bytes 8388608
  17.0 11.4 %slice-start.1 = ((s8[14155776]{0:T(1024)(128)(4,1)}), s8[4194304]{0:T(1024)(128)(4,1)S(1)}, s32[]{:S(2)}) async-start(s8[14155776]{0:T(1024)(128)(4,1)} %bitcast.10), calls=%async_computation.1 | async-start | bytes 8388608
  17.0 11.4 %slice-start.2 = ((s8[14155776]{0:T(1024)(128)(4,1)}), s8[4194304]{0:T(1024)(128)(4,1)S(1)}, s32[]{:S(2)}) async-start(s8[14155776]{0:T(1024)(128)(4,1)} %bitcast.10), calls=%async_computation.2 | async-start | bytes 8388608
  17.0 11.4 %slice-start.3 = ((s8[14155776]{0:T(1024)(128)(4,1)}), s8[1572864]{0:T(1024)(128)(4,1)S(1)}, s32[]{:S(2)}) async-start(s8[14155776]{0:T(1024)(128)(4,1)} %bitcast.10), calls=%async_computation.3 | async-start | bytes 3145728
  25.5 5.8 %collective-permute-start.3 = (bf16[2,1,64,512]{3,2,1,0:T(8,128)(2,1)S(1)}, bf16[2,1,64,512]{3,2,1,0:T(8,128)(2,1)S(1)}, u32[]{:S(2)}, u32[]{:S(2)}) collective-permute-start(bf16[2,1,64,512]{3,2,1,0:T(8,128)(2,1)S(1)} %get-tuple-element.42), channel_id=1, source_target_pairs={{0,1},{1,0},{2,3},{3,2},{4,5},{5,4},{6,7},{7,6},{8,9},{9,8},{10,11... | collective-permute-start | bytes 393224 | tf_op jit(solution)/shard_map/ppermute | solution.py:431
  25.6 7.6 %collective-permute-start.4 = (bf16[2,1,64,512]{3,2,1,0:T(8,128)(2,1)S(1)}, bf16[2,1,64,512]{3,2,1,0:T(8,128)(2,1)S(1)}, u32[]{:S(2)}, u32[]{:S(2)}) collective-permute-start(bf16[2,1,64,512]{3,2,1,0:T(8,128)(2,1)S(1)} %get-tuple-element.41), channel_id=1, source_target_pairs={{0,0},{1,2},{2,1},{3,4},{4,3},{5,6},{6,5},{7,7},{8,8},{9,10},{10,9... | collective-permute-start | bytes 393224 | tf_op jit(solution)/shard_map/ppermute | solution.py:432
  30.5 11.3 %collective-permute-start.5 = (bf16[2,2,64,512]{3,2,1,0:T(8,128)(2,1)S(1)}, bf16[2,2,64,512]{3,2,1,0:T(8,128)(2,1)S(1)}, u32[]{:S(2)}, u32[]{:S(2)}) collective-permute-start(bf16[2,2,64,512]{3,2,1,0:T(8,128)(2,1)S(1)} %shard_map.88), channel_id=1, source_target_pairs={{0,8},{8,16},{16,24},{24,0},{1,9},{9,17},{17,25},{25,1},{2,10},{10... | collective-permute-start | bytes 786440 | tf_op jit(solution)/shard_map/ppermute | solution.py:540
  35.3 9.6 %collective-permute-start.6 = (bf16[2,2,64,512]{3,2,1,0:T(8,128)(2,1)S(1)}, bf16[2,2,64,512]{3,2,1,0:T(8,128)(2,1)S(1)}, u32[]{:S(2)}, u32[]{:S(2)}) collective-permute-start(bf16[2,2,64,512]{3,2,1,0:T(8,128)(2,1)S(1)} %shard_map.89), channel_id=1, source_target_pairs={{0,8},{8,16},{16,24},{1,9},{9,17},{17,25},{2,10},{10,18},{18,26},{... | collective-permute-start | bytes 786440 | tf_op jit(solution)/shard_map/ppermute | solution.py:548

commit v2 on v1

--- a/solution.py
+++ b/solution.py
@@ -85,7 +85,7 @@
     pairs = [
         (feat_hbm.at[:, pl.ds((height - 1) * use_last, 1)], ref)
         for ref, use_last in ((far_ref, odd), (near_ref, 1 - odd))
-    ] + [(gain_hbm, gain_ref), (feat_hbm.at[0:1], start_ref)]
+    ] + [(gain_hbm, gain_ref), (feat_hbm.at[pl.ds(feat_hbm.shape[0] - 2, 1)], start_ref)]
     copies = [pltpu.make_async_copy(src, dst, sem.at[n]) for n, (src, dst) in enumerate(pairs)]
     for copy in copies:
         copy.start()
@@ -99,32 +99,38 @@
 ):
     _, height, _, channels = start_ref.shape
     frames = x_ref.shape[0]
+    order = [frames - 2, frames - 1, *range(frames - 2)]
     feat_copies = [
-        pltpu.make_async_copy(feat_hbm.at[f], feat_ref.at[f - 1], feat_sem.at[f - 1])
-        for f in range(1, frames)
+        pltpu.make_async_copy(feat_hbm.at[f], feat_ref.at[n], feat_sem.at[n])
+        for n, f in enumerate(order[1:])
     ]
     w_copies = [pltpu.make_async_copy(w_hbm.at[a], w_ref.at[a], w_sem.at[a]) for a in range(3)]
     down_copy = pltpu.make_async_copy(down_hbm, down_ref, down_sem)
     for copy in (*feat_copies, *w_copies, down_copy):
         copy.start()
-    clear_pads(pad_ref)
+    for n in range(2):
+        clear_pads(pad_ref.at[n])
     gain = gain_ref[...]
-
-    for f in range(frames):
-        frame_ref = start_ref.at[0] if f == 0 else feat_ref.at[f - 1]
-        if f > 0:
-            feat_copies[f - 1].wait()
+    frame_refs = [start_ref.at[0], *(feat_ref.at[n] for n in range(frames - 1))]
+
+    def rows_of(n, h, slot):
+        f = order[n]
+
+        def store(t, value):
+            x_ref[f, t, pl.ds(h + 1, step)] = value.astype(jnp.bfloat16)
+
+        def residual(r, value):
+            res_ref[f, r, pl.ds(h, step)] = value
+
+        values = frame_refs[n][pl.ds(h, step)]
+        prepare(values, gain, raw_ref.at[slot], pad_ref.at[slot], store, residual)
+
+    for n in range(2):
+        if n > 0:
+            feat_copies[n - 1].wait()
 
         def body(index, carry):
-            h = index * step
-
-            def store(t, value):
-                x_ref[f, t, pl.ds(h + 1, step)] = value.astype(jnp.bfloat16)
-
-            def residual(r, value):
-                res_ref[f, r, pl.ds(h, step)] = value
-
-            prepare(frame_ref[pl.ds(h, step)], gain, raw_ref, pad_ref, store, residual)
+            rows_of(n, index * step, 0)
             return carry
 
         lax.fori_loop(0, height // step, body, 0)
@@ -141,26 +147,48 @@
 
         lax.fori_loop(0, 3, combine, 0)
 
-    down_copy.wait()
-    rows = 32
-
-    def fold(index, carry):
-        r = pl.multiple_of(index * rows, rows)
-        parts = [down_ref[s, pl.ds(r, rows), :].astype(jnp.float32) for s in range(8)]
+    for copy in (*feat_copies[1:], down_copy):
+        copy.wait()
+    rows, lanes = 16, 256
+
+    def fold(r, q):
+        parts = [down_ref[s, r : r + rows, q : q + lanes].astype(jnp.float32) for s in range(8)]
         for bit in (4, 2):
             parts = [
                 parts[s] + parts[s + bit] if not s & bit else parts[s - bit] - parts[s]
                 for s in range(8)
             ]
         for s in range(8):
-            v_ref[s, pl.ds(r, rows), :] = parts[s].astype(jnp.bfloat16)
-        return carry
-
-    lax.fori_loop(0, channels // rows, fold, 0)
+            v_ref[s, r : r + rows, q : q + lanes] = parts[s].astype(jnp.bfloat16)
+
     inner, _ = groups_of(height // 2)
-    for deep_rows in inner:
-        conv_rows(frames // 2, deep_rows, x_ref, w_ref, g_ref, None, lev_ref)
-        conv_rows(frames // 2 - 1, deep_rows, x_ref, w_ref, g_ref, res_ref, own_lev_ref, (0,))
+    norms = [
+        functools.partial(rows_of, n, h, (h // step) % 2)
+        for n in range(2, frames)
+        for h in range(0, height, step)
+    ]
+    interleave(
+        [
+            one
+            for deep_rows in inner
+            for one in conv_steps(frames // 2, deep_rows, x_ref, w_ref, g_ref, None, lev_ref)
+        ],
+        norms,
+    )
+    interleave(
+        [
+            one
+            for deep_rows in inner
+            for one in conv_steps(
+                frames // 2 - 1, deep_rows, x_ref, w_ref, g_ref, res_ref, own_lev_ref
+            )
+        ],
+        [
+            functools.partial(fold, r, q)
+            for r in range(0, channels, rows)
+            for q in range(0, down_ref.shape[-1], lanes)
+        ],
+    )
 
 
 def groups_of(deep_rows):
@@ -168,29 +196,28 @@
     return [tuple(inner[n : n + 2]) for n in range(0, len(inner), 2)], (0, deep_rows - 1)
 
 
-def conv_rows(pair, deep_rows, x_ref, w_ref, g_ref, res_ref, lev_ref, parts=(0, 1)):
+def conv_steps(pair, deep_rows, x_ref, w_ref, g_ref, res_ref, lev_ref):
     frames, _, _, half, channels = x_ref.shape
-    for i in parts:
-        f = 2 * pair + i
-        taps = [a for a in range(3) if 0 <= f + a - 2 < frames]
-        sums = []
-        for t in range(4):
-            total = None
-            for a in taps:
-                for b in range(3):
-                    rows = jnp.concatenate(
-                        [
-                            x_ref[f + a - 2, t, 2 * h + b : 2 * h + b + 2].reshape(
-                                2 * half, channels
-                            )
-                            for h in deep_rows
-                        ],
-                        0,
-                    )
-                    weight = (w_ref[a, b, 0], g_ref[a, b, 0], g_ref[a, b, 1], w_ref[a, b, 2])[t]
-                    part = dot(rows, weight)
-                    total = part if total is None else total + part
-            sums.append(total)
+
+    def chain(sums, f, t):
+        total = None
+        for a in range(3):
+            if not 0 <= f + a - 2 < frames:
+                continue
+            for b in range(3):
+                rows = jnp.concatenate(
+                    [
+                        x_ref[f + a - 2, t, 2 * h + b : 2 * h + b + 2].reshape(2 * half, channels)
+                        for h in deep_rows
+                    ],
+                    0,
+                )
+                weight = (w_ref[a, b, 0], g_ref[a, b, 0], g_ref[a, b, 1], w_ref[a, b, 2])[t]
+                part = dot(rows, weight)
+                total = part if total is None else total + part
+        sums.append(total)
+
+    def finish(sums, i):
         pieces = (sums[0] - sums[3] + sums[1], sums[0] + sums[3] + sums[2])
         for r in range(2):
             for n, h in enumerate(deep_rows):
@@ -198,8 +225,31 @@
                     at = (2 * n + j) * half
                     level = pieces[r][at : at + half]
                     if res_ref is not None:
-                        level = level + res_ref[f, r, 2 * h + j]
+                        level = level + res_ref[2 * pair + i, r, 2 * h + j]
                     lev_ref[4 * i + 2 * j + r, h] = level.astype(jnp.bfloat16)
+
+    steps = []
+    for i in range(2):
+        sums = []
+        for t in range(4):
+            steps.append(functools.partial(chain, sums, 2 * pair + i, t))
+        steps.append(functools.partial(finish, sums, i))
+    return steps
+
+
+def conv_rows(*args):
+    for step in conv_steps(*args):
+        step()
+
+
+def interleave(matrix_steps, vector_steps):
+    done = 0
+    for n, step in enumerate(matrix_steps):
+        step()
+        upto = len(vector_steps) * (n + 1) // len(matrix_steps)
+        for other in vector_steps[done:upto]:
+            other()
+        done = upto
 
 
 def project(lev_ref, v_ref):
@@ -252,10 +302,8 @@
     for pair in reversed(range(deep_frames)):
         last = pair == deep_frames - 1
         level = last_lev_ref if last else lev_ref.at[pair % 2]
-        for deep_rows in inner:
-            parts = (1,) if last else (0, 1)
-            conv_rows(pair, deep_rows, x_ref, w_ref, g_ref, res_ref, level, parts)
-        conv_rows(pair, outer, x_ref, w_ref, g_ref, res_ref, level)
+        for deep_rows in (outer,) if last else (*inner, outer):
+            conv_rows(pair, deep_rows, x_ref, w_ref, g_ref, res_ref, level)
         injected = [
             lax.dot_general(
                 wav_ref[pair, :, h, :],
@@ -478,8 +526,8 @@
         (
             pltpu.VMEM((frames - 1, height, width, channels), bf16),
             pltpu.VMEM(down_weight.shape, bf16),
-            pltpu.VMEM((step, channels // 128, width, 128), f32),
-            pltpu.VMEM((2, step, half + 2 * PAD, channels), f32),
+            pltpu.VMEM((2, step, channels // 128, width, 128), f32),
+            pltpu.VMEM((2, 2, step, half + 2 * PAD, channels), f32),
             sem((frames - 1,)),
             sem(()),
             sem((3,)),

time: 46 us -> 44.9 us (0.976)
  the two profiles are of different devices: /device:TPU:20 before, /device:TPU:27 now
where the time goes in v2:
time: 44.9 us; the launch traced here: 44.8 us
  Pallas kernels  27.9 us (62%)
  starting transfers between devices  10.6 us (24%)
  waiting for transfers between devices  5.85 us (13%)
    pallas_call x9, Pallas kernels, call(): pl.pallas_call(kernel, out_shape=outs, in_specs=[pl.BlockSpec(memory_spac...  27.9 us
    ppermute x2, starting transfers between devices, exchange(): far = lax.ppermute(far, 'rows', routes[1])  6.06 us
    ppermute x1, waiting for transfers between devices, on_device(): outer = lax.ppermute(outer, 'tm', chain('tm', WRAPS[2]))  4.22 us
    ppermute x1, starting transfers between devices, on_device(): inner = lax.ppermute(inner, 'tm', chain('tm', WRAPS[1]))  1.86 us
    ppermute x1, waiting for transfers between devices, on_device(): carried = lax.ppermute(carry, 'tm', chain('tm', WRAPS[0]))  1.48 us
    ppermute x1, starting transfers between devices, on_device(): outer = lax.ppermute(outer, 'tm', chain('tm', WRAPS[2]))  1.29 us
    ppermute x2, starting transfers between devices, exchange(): near = lax.ppermute(near, 'rows', routes[0])  1.2 us
  transfers between devices with their start and end apart: 7, of which 3 were waited for; matrix products, arithmetic and copies ran while one was open for 0% of the time, Pallas kernels for 51%

profile of v2, /device:TPU:27, one launch (start us, length us, event | category | flops | bytes accessed | tf_op | source)
XLA Modules:
  0.0 44.8 jit_solution(17916753647372648924)
XLA Ops:
  0.0 1.3 %shard_map.82 = (bf16[4,1,128,256]{3,2,1,0:T(8,128)(2,1)S(1)}, bf16[4,1,128,256]{3,2,1,0:T(8,128)(2,1)S(1)}, bf16[1,8,128,256]{3,2,1,0:T(8,128)(2,1)S(1)}, f32[1,256]{1,0:T(1,128)S(1)}) custom-call(bf16[4,8,128,256]{3,2,1,0:T(8,128)(2,1)} %feat_hbm.3, f32[1,256]{1,0:T(1,128)} %bitcast.14), custom_call_target="tpu_custom_call" | custom-call | bytes 2098176 | tf_op jit(solution)/shard_map/pallas_call | solution.py:26
  1.3 0.7 %collective-permute-start = (bf16[4,1,128,256]{3,2,1,0:T(8,128)(2,1)S(1)}, bf16[4,1,128,256]{3,2,1,0:T(8,128)(2,1)S(1)}, u32[]{:S(2)}, u32[]{:S(2)}) collective-permute-start(bf16[4,1,128,256]{3,2,1,0:T(8,128)(2,1)S(1)} %get-tuple-element.28), channel_id=1, source_target_pairs={{0,1},{1,0},{2,3},{3,2},{4,5},{5,4},{6,7},{7,6},{8,9},{9,8},{10,11... | collective-permute-start | bytes 786440 | tf_op jit(solution)/shard_map/ppermute | solution.py:479
  2.0 3.0 %collective-permute-start.1 = (bf16[4,1,128,256]{3,2,1,0:T(8,128)(2,1)S(1)}, bf16[4,1,128,256]{3,2,1,0:T(8,128)(2,1)S(1)}, u32[]{:S(2)}, u32[]{:S(2)}) collective-permute-start(bf16[4,1,128,256]{3,2,1,0:T(8,128)(2,1)S(1)} %get-tuple-element.29), channel_id=1, source_target_pairs={{0,0},{1,2},{2,1},{3,4},{4,3},{5,6},{6,5},{7,7},{8,8},{9,10},{10,9... | collective-permute-start | bytes 786440 | tf_op jit(solution)/shard_map/ppermute | solution.py:480
  5.0 8.1 %shard_map.83 = (bf16[4,4,10,64,256]{4,3,2,1,0:T(8,128)(2,1)S(1)}, f32[4,2,8,64,256]{4,3,2,1,0:T(8,128)S(1)}, bf16[8,256,512]{2,1,0:T(8,128)(2,1)S(1)}, bf16[3,3...) custom-call(bf16[1,8,128,256]{3,2,1,0:T(8,128)(2,1)S(1)} %get-tuple-, ...), custom_call_target="tpu_custom_call" | custom-call | flops 5000000000 | bytes 8258560 | tf_op jit(solution)/shard_map/pallas_call | solution.py:26
  13.2 0.0 collective-permute-done.near_ref
  13.2 0.0 collective-permute-done.1.far_ref
  13.2 0.0 copy-start
  13.2 0.0 copy-start.1
  13.2 0.0 copy-start.2
  13.2 2.4 %shard_map.84 = (bf16[4,4,10,64,256]{4,3,2,1,0:T(8,128)(2,1)S(1)}, bf16[8,4,64,256]{3,2,1,0:T(8,128)(2,1)S(1)}, bf16[4,64,512]{2,1,0:T(8,128)(2,1)S(1)}) custom-call(bf16[4,4,10,64,256]{4,3,2,1,0:T(8,128)(2,1)S(1)} %get-tuple-element.26.x_in, bf16[8,4,64,256]{3,2,1,0:T(8,128)(2,1)S(1)} %get-tuple-element.27.lev_in, ...), custom_call_target="tpu_custom_call", output_to_operand_aliasing={{0}: (0, {}), {1}: (1, {})} | custom-call | flops 2952790016 | bytes 14812160 | tf_op jit(solution)/shard_map/pallas_call | solution.py:26
  15.6 0.2 collective-permute-start.2
  15.9 0.0 slice-start
  15.9 0.0 copy-done
  15.9 0.0 copy-done.1
  15.9 0.0 copy-done.2
  15.9 0.0 slice-start.1
  15.9 0.0 slice-start.2
  15.9 0.0 slice-start.3
  15.9 6.7 %shard_map.85 = (bf16[8,4,64,256]{3,2,1,0:T(8,128)(2,1)S(1)}, f32[4,64,512]{2,1,0:T(8,128)S(1)}, f32[4,64,512]{2,1,0:T(8,128)S(1)}, bf16[4,64,512]{2,1,0:T(8,128)(2,1)S(1)}) custom-call(bf16[8,4,64,256]{3,2,1,0:T(8,128)(2,1)S(1)} %get-tuple-element.25.lev_in, ...), custom_call_target="tpu_custom_call", output_to_operand_aliasing={{0}: (0, {})} | custom-call | flops 8321499136 | bytes 18532352 | tf_op jit(solution)/shard_map/pallas_call | solution.py:26
  22.7 1.5 %collective-permute-done.2.carried_ref = bf16[4,64,512]{2,1,0:T(8,128)(2,1)S(1)} collective-permute-done((bf16[4,64,512]{2,1,0:T(8,128)(2,1)S(1)}, bf16[4,64,512]{2,1,0:T(8,128)(2,1)S(1)}, u32[]{:S(2)}, u32[]{:S(2)}) %collective-permute-start.2) | collective-permute-done | bytes 262176 | tf_op jit(solution)/shard_map/ppermute | solution.py:552
  24.1 0.3 shard_map.86
  24.5 0.5 %collective-permute-start.3 = (bf16[2,1,64,512]{3,2,1,0:T(8,128)(2,1)S(1)}, bf16[2,1,64,512]{3,2,1,0:T(8,128)(2,1)S(1)}, u32[]{:S(2)}, u32[]{:S(2)}) collective-permute-start(bf16[2,1,64,512]{3,2,1,0:T(8,128)(2,1)S(1)} %get-tuple-element.42), channel_id=1, source_target_pairs={{0,1},{1,0},{2,3},{3,2},{4,5},{5,4},{6,7},{7,6},{8,9},{9,8},{10,11... | collective-permute-start | bytes 393224 | tf_op jit(solution)/shard_map/ppermute | solution.py:479
  25.0 3.0 %collective-permute-start.4 = (bf16[2,1,64,512]{3,2,1,0:T(8,128)(2,1)S(1)}, bf16[2,1,64,512]{3,2,1,0:T(8,128)(2,1)S(1)}, u32[]{:S(2)}, u32[]{:S(2)}) collective-permute-start(bf16[2,1,64,512]{3,2,1,0:T(8,128)(2,1)S(1)} %get-tuple-element.41), channel_id=1, source_target_pairs={{0,0},{1,2},{2,1},{3,4},{4,3},{5,6},{6,5},{7,7},{8,8},{9,10},{10,9... | collective-permute-start | bytes 393224 | tf_op jit(solution)/shard_map/ppermute | solution.py:480
  28.0 0.0 slice-done
  28.0 0.0 slice-done.1
  28.0 0.0 slice-done.2
  28.1 0.0 slice-done.3
  28.1 2.1 %shard_map.88 = bf16[2,2,64,512]{3,2,1,0:T(8,128)(2,1)S(1)} custom-call(bf16[4,64,512]{2,1,0:T(8,128)(2,1)S(1)} %get-tuple-element.37.refs_0_.before_ref, bf16[4,64,512]{2,1,0:T(8,128)(2,1)S(1)} %get-tuple-element.38.refs_1_.latest_ref, bf16[3,3,3,512,512]{4,3,2,1,0:T(8,128)(2,1)S(1)} %bitcast.11), custom_call_target="tpu_custom_call" | custom-call | flops 1811939328 | bytes 14680064 | tf_op jit(solution)/shard_map/pallas_call | solution.py:26
  30.1 1.9 %collective-permute-start.5 = (bf16[2,2,64,512]{3,2,1,0:T(8,128)(2,1)S(1)}, bf16[2,2,64,512]{3,2,1,0:T(8,128)(2,1)S(1)}, u32[]{:S(2)}, u32[]{:S(2)}) collective-permute-start(bf16[2,2,64,512]{3,2,1,0:T(8,128)(2,1)S(1)} %shard_map.88), channel_id=1, source_target_pairs={{0,8},{8,16},{16,24},{24,0},{1,9},{9,17},{17,25},{25,1},{2,10},{10... | collective-permute-start | bytes 786440 | tf_op jit(solution)/shard_map/ppermute | solution.py:588
  32.0 0.0 collective-permute-done.3.refs_4_.near_ref
  32.0 0.1 collective-permute-done.4.refs_5_.far_ref
  32.1 2.1 %shard_map.89 = bf16[2,2,64,512]{3,2,1,0:T(8,128)(2,1)S(1)} custom-call(bf16[4,64,512]{2,1,0:T(8,128)(2,1)S(1)} %get-tuple-element.37.refs_0_.before_ref, bf16[4,64,512]{2,1,0:T(8,128)(2,1)S(1)} %get-tuple-element.38.refs_1_.latest_ref, bf16[2,1,64,512]{3,2,1,0:T(8,128)(2,1)S(1)} %collective-permute-done.3.refs_4_.near_ref, ...), custom_call_target="tpu_custom_call" | custom-call | flops 1811939328 | bytes 14942208 | tf_op jit(solution)/shard_map/pallas_call | solution.py:26
  34.2 1.3 %collective-permute-start.6 = (bf16[2,2,64,512]{3,2,1,0:T(8,128)(2,1)S(1)}, bf16[2,2,64,512]{3,2,1,0:T(8,128)(2,1)S(1)}, u32[]{:S(2)}, u32[]{:S(2)}) collective-permute-start(bf16[2,2,64,512]{3,2,1,0:T(8,128)(2,1)S(1)} %shard_map.89), channel_id=1, source_target_pairs={{0,8},{8,16},{16,24},{1,9},{9,17},{17,25},{2,10},{10,18},{18,26},{... | collective-permute-start | bytes 786440 | tf_op jit(solution)/shard_map/ppermute | solution.py:596
  35.5 4.1 %shard_map.87.own_ref = f32[2,4,64,512]{3,2,1,0:T(8,128)S(1)} custom-call(bf16[4,64,512]{2,1,0:T(8,128)(2,1)S(1)} %get-tuple-element.37.refs_0_.before_ref, bf16[4,64,512]{2,1,0:T(8,128)(2,1)S(1)} %get-tuple-element.38.refs_1_.latest_ref, f32[4,64,512]{2,1,0:T(8,128)S(1)} %get-tuple-element.39.refs_2_, f32[4,64,512]{2,1,0:T(8,128)S(1)} %get-tuple-element.40.refs_3_, ...), custom_call_target="tpu_custom_call" | custom-call | flops 3623878656 | bytes 15990784 | tf_op jit(solution)/shard_map/pallas_call | solution.py:26
  39.6 0.0 collective-permute-done.5.inner_ref
  39.6 4.2 %collective-permute-done.6.outer_ref = bf16[2,2,64,512]{3,2,1,0:T(8,128)(2,1)S(1)} collective-permute-done((bf16[2,2,64,512]{3,2,1,0:T(8,128)(2,1)S(1)}, bf16[2,2,64,512]{3,2,1,0:T(8,128)(2,1)S(1)}, u32[]{:S(2)}, u32[]{:S(2)}) %collective-permute-start.6) | collective-permute-done | bytes 262176 | tf_op jit(solution)/shard_map/ppermute | solution.py:596
  43.8 0.9 %shard_map.90 = bf16[2,4,64,512]{3,2,1,0:T(8,128)(2,1)} custom-call(f32[2,4,64,512]{3,2,1,0:T(8,128)S(1)} %shard_map.87.own_ref, bf16[2,2,64,512]{3,2,1,0:T(8,128)(2,1)S(1)} %collective-permute-done.5.inner_ref, bf16[2,2,64,512]{3,2,1,0:T(8,128)(2,1)S(1)} %collective-permute-done.6.outer_ref), custom_call_target="tpu_custom_call" | custom-call | bytes 1572864 | tf_op jit(solution)/shard_map/pallas_call | solution.py:26
  (3 shorter events, 0.1 us)
Async XLA Ops:
  1.3 11.9 %collective-permute-start = (bf16[4,1,128,256]{3,2,1,0:T(8,128)(2,1)S(1)}, bf16[4,1,128,256]{3,2,1,0:T(8,128)(2,1)S(1)}, u32[]{:S(2)}, u32[]{:S(2)}) collective-permute-start(bf16[4,1,128,256]{3,2,1,0:T(8,128)(2,1)S(1)} %get-tuple-element.28), channel_id=1, source_target_pairs={{0,1},{1,0},{2,3},{3,2},{4,5},{5,4},{6,7},{7,6},{8,9},{9,8},{10,11... | collective-permute-start | bytes 786440 | tf_op jit(solution)/shard_map/ppermute | solution.py:479
  2.0 11.2 %collective-permute-start.1 = (bf16[4,1,128,256]{3,2,1,0:T(8,128)(2,1)S(1)}, bf16[4,1,128,256]{3,2,1,0:T(8,128)(2,1)S(1)}, u32[]{:S(2)}, u32[]{:S(2)}) collective-permute-start(bf16[4,1,128,256]{3,2,1,0:T(8,128)(2,1)S(1)} %get-tuple-element.29), channel_id=1, source_target_pairs={{0,0},{1,2},{2,1},{3,4},{4,3},{5,6},{6,5},{7,7},{8,8},{9,10},{10,9... | collective-permute-start | bytes 786440 | tf_op jit(solution)/shard_map/ppermute | solution.py:480
  13.2 2.7 %copy-start = (f32[512]{0:T(512)S(1)}, f32[512]{0:T(512)}, u32[]{:S(2)}) copy-start(f32[512]{0:T(512)} %param.14) | copy-start | bytes 6148
  13.2 2.7 %copy-start.1 = (bf16[2,24,4,64]{3,2,1,0:T(4,128)(2,1)S(1)}, bf16[2,24,4,64]{3,2,1,0:T(4,128)(2,1)}, u32[]{:S(2)}) copy-start(bf16[2,24,4,64]{3,2,1,0:T(4,128)(2,1)} %wav_ref.1) | copy-start | bytes 73732
  13.2 2.7 %copy-start.2 = (bf16[24,512]{1,0:T(8,128)(2,1)S(1)}, bf16[24,512]{1,0:T(8,128)(2,1)}, u32[]{:S(2)}) copy-start(bf16[24,512]{1,0:T(8,128)(2,1)} %inj_ref.1) | copy-start | bytes 73732
  15.6 8.5 %collective-permute-start.2 = (bf16[4,64,512]{2,1,0:T(8,128)(2,1)S(1)}, bf16[4,64,512]{2,1,0:T(8,128)(2,1)S(1)}, u32[]{:S(2)}, u32[]{:S(2)}) collective-permute-start(bf16[4,64,512]{2,1,0:T(8,128)(2,1)S(1)} %get-tuple-element.36), channel_id=1, source_target_pairs={{0,8},{8,16},{16,24},{24,0},{1,9},{9,17},{17,25},{25,1},{2,10},{10... | collective-permute-start | bytes 786440 | tf_op jit(solution)/shard_map/ppermute | solution.py:552
  15.9 12.2 %slice-start = ((s8[14155776]{0:T(1024)(128)(4,1)}), s8[4194304]{0:T(1024)(128)(4,1)S(1)}, s32[]{:S(2)}) async-start(s8[14155776]{0:T(1024)(128)(4,1)} %bitcast.10), calls=%async_computation | async-start | bytes 8388608
  15.9 12.1 %slice-start.1 = ((s8[14155776]{0:T(1024)(128)(4,1)}), s8[4194304]{0:T(1024)(128)(4,1)S(1)}, s32[]{:S(2)}) async-start(s8[14155776]{0:T(1024)(128)(4,1)} %bitcast.10), calls=%async_computation.1 | async-start | bytes 8388608
  15.9 12.1 %slice-start.2 = ((s8[14155776]{0:T(1024)(128)(4,1)}), s8[4194304]{0:T(1024)(128)(4,1)S(1)}, s32[]{:S(2)}) async-start(s8[14155776]{0:T(1024)(128)(4,1)} %bitcast.10), calls=%async_computation.2 | async-start | bytes 8388608
  15.9 12.1 %slice-start.3 = ((s8[14155776]{0:T(1024)(128)(4,1)}), s8[1572864]{0:T(1024)(128)(4,1)S(1)}, s32[]{:S(2)}) async-start(s8[14155776]{0:T(1024)(128)(4,1)} %bitcast.10), calls=%async_computation.3 | async-start | bytes 3145728
  24.5 7.5 %collective-permute-start.3 = (bf16[2,1,64,512]{3,2,1,0:T(8,128)(2,1)S(1)}, bf16[2,1,64,512]{3,2,1,0:T(8,128)(2,1)S(1)}, u32[]{:S(2)}, u32[]{:S(2)}) collective-permute-start(bf16[2,1,64,512]{3,2,1,0:T(8,128)(2,1)S(1)} %get-tuple-element.42), channel_id=1, source_target_pairs={{0,1},{1,0},{2,3},{3,2},{4,5},{5,4},{6,7},{7,6},{8,9},{9,8},{10,11... | collective-permute-start | bytes 393224 | tf_op jit(solution)/shard_map/ppermute | solution.py:479
  25.0 7.2 %collective-permute-start.4 = (bf16[2,1,64,512]{3,2,1,0:T(8,128)(2,1)S(1)}, bf16[2,1,64,512]{3,2,1,0:T(8,128)(2,1)S(1)}, u32[]{:S(2)}, u32[]{:S(2)}) collective-permute-start(bf16[2,1,64,512]{3,2,1,0:T(8,128)(2,1)S(1)} %get-tuple-element.41), channel_id=1, source_target_pairs={{0,0},{1,2},{2,1},{3,4},{4,3},{5,6},{6,5},{7,7},{8,8},{9,10},{10,9... | collective-permute-start | bytes 393224 | tf_op jit(solution)/shard_map/ppermute | solution.py:480
  30.1 9.5 %collective-permute-start.5 = (bf16[2,2,64,512]{3,2,1,0:T(8,128)(2,1)S(1)}, bf16[2,2,64,512]{3,2,1,0:T(8,128)(2,1)S(1)}, u32[]{:S(2)}, u32[]{:S(2)}) collective-permute-start(bf16[2,2,64,512]{3,2,1,0:T(8,128)(2,1)S(1)} %shard_map.88), channel_id=1, source_target_pairs={{0,8},{8,16},{16,24},{24,0},{1,9},{9,17},{17,25},{25,1},{2,10},{10... | collective-permute-start | bytes 786440 | tf_op jit(solution)/shard_map/ppermute | solution.py:588
  34.2 9.6 %collective-permute-start.6 = (bf16[2,2,64,512]{3,2,1,0:T(8,128)(2,1)S(1)}, bf16[2,2,64,512]{3,2,1,0:T(8,128)(2,1)S(1)}, u32[]{:S(2)}, u32[]{:S(2)}) collective-permute-start(bf16[2,2,64,512]{3,2,1,0:T(8,128)(2,1)S(1)} %shard_map.89), channel_id=1, source_target_pairs={{0,8},{8,16},{16,24},{1,9},{9,17},{17,25},{2,10},{10,18},{18,26},{... | collective-permute-start | bytes 786440 | tf_op jit(solution)/shard_map/ppermute | solution.py:596

commit v3 on v2

--- a/solution.py
+++ b/solution.py
@@ -99,14 +99,14 @@
 ):
     _, height, _, channels = start_ref.shape
     frames = x_ref.shape[0]
-    order = [frames - 2, frames - 1, *range(frames - 2)]
+    order = [frames - 2, frames - 1, *reversed(range(frames - 2))]
     feat_copies = [
         pltpu.make_async_copy(feat_hbm.at[f], feat_ref.at[n], feat_sem.at[n])
         for n, f in enumerate(order[1:])
     ]
     w_copies = [pltpu.make_async_copy(w_hbm.at[a], w_ref.at[a], w_sem.at[a]) for a in range(3)]
     down_copy = pltpu.make_async_copy(down_hbm, down_ref, down_sem)
-    for copy in (*feat_copies, *w_copies, down_copy):
+    for copy in (feat_copies[0], *w_copies, *feat_copies[1:], down_copy):
         copy.start()
     for n in range(2):
         clear_pads(pad_ref.at[n])
@@ -135,20 +135,16 @@
 
         lax.fori_loop(0, height // step, body, 0)
 
-    for a in range(3):
-        w_copies[a].wait()
-
-        def combine(b, carry):
-            first, mid, last = (w_ref[a, b, c].astype(jnp.float32) for c in range(3))
-            outer = first + last
-            g_ref[a, b, 0] = (outer + mid).astype(jnp.bfloat16)
-            g_ref[a, b, 1] = (outer - mid).astype(jnp.bfloat16)
-            return carry
-
-        lax.fori_loop(0, 3, combine, 0)
-
-    for copy in (*feat_copies[1:], down_copy):
+    for copy in w_copies:
         copy.wait()
+
+    def combine(a, b, r):
+        rows = slice(r, r + 32)
+        first, mid, last = (w_ref[a, b, c, rows, :].astype(jnp.float32) for c in range(3))
+        outer = first + last
+        g_ref[a, b, 0, rows, :] = (outer + mid).astype(jnp.bfloat16)
+        g_ref[a, b, 1, rows, :] = (outer - mid).astype(jnp.bfloat16)
+
     rows, lanes = 16, 256
 
     def fold(r, q):
@@ -162,27 +158,37 @@
             v_ref[s, r : r + rows, q : q + lanes] = parts[s].astype(jnp.bfloat16)
 
     inner, _ = groups_of(height // 2)
-    norms = [
-        functools.partial(rows_of, n, h, (h // step) % 2)
-        for n in range(2, frames)
-        for h in range(0, height, step)
-    ]
+
+    def norms(first, last):
+        return [
+            functools.partial(rows_of, n, h, (h // step) % 2)
+            for n in range(first, last)
+            for h in range(0, height, step)
+        ]
+
+    def steps(pair, level_ref, residual_ref, parts):
+        both = [
+            conv_steps(pair, deep_rows, x_ref, w_ref, g_ref, residual_ref, level_ref, parts)
+            for deep_rows in inner
+        ]
+        return [sum(some, []) for some in zip(*both)]
+
+    early, late = steps(frames // 2, lev_ref, None, (0, 1))
     interleave(
+        early,
         [
-            one
-            for deep_rows in inner
-            for one in conv_steps(frames // 2, deep_rows, x_ref, w_ref, g_ref, None, lev_ref)
+            functools.partial(combine, a, b, r)
+            for a in range(3)
+            for b in range(3)
+            for r in range(0, channels, 32)
         ],
-        norms,
-    )
+    )
+    for copy in (*feat_copies[1:], down_copy):
+        copy.wait()
+    interleave(late, norms(2, 3))
+    interleave(sum(steps(frames // 2 - 1, own_lev_ref, res_ref, (1,)), []), norms(3, frames))
     interleave(
-        [
-            one
-            for deep_rows in inner
-            for one in conv_steps(
-                frames // 2 - 1, deep_rows, x_ref, w_ref, g_ref, res_ref, own_lev_ref
-            )
-        ],
+        sum(steps(frames // 2 - 1, own_lev_ref, res_ref, (0,)), []),
         [
             functools.partial(fold, r, q)
             for r in range(0, channels, rows)
@@ -196,7 +202,7 @@
     return [tuple(inner[n : n + 2]) for n in range(0, len(inner), 2)], (0, deep_rows - 1)
 
 
-def conv_steps(pair, deep_rows, x_ref, w_ref, g_ref, res_ref, lev_ref):
+def conv_steps(pair, deep_rows, x_ref, w_ref, g_ref, res_ref, lev_ref, parts=(0, 1)):
     frames, _, _, half, channels = x_ref.shape
 
     def chain(sums, f, t):
@@ -215,7 +221,7 @@
                 weight = (w_ref[a, b, 0], g_ref[a, b, 0], g_ref[a, b, 1], w_ref[a, b, 2])[t]
                 part = dot(rows, weight)
                 total = part if total is None else total + part
-        sums.append(total)
+        sums[t] = total
 
     def finish(sums, i):
         pieces = (sums[0] - sums[3] + sums[1], sums[0] + sums[3] + sums[2])
@@ -228,18 +234,20 @@
                         level = level + res_ref[2 * pair + i, r, 2 * h + j]
                     lev_ref[4 * i + 2 * j + r, h] = level.astype(jnp.bfloat16)
 
-    steps = []
+    early, late = [], []
+    for i in parts:
+        sums = {}
+        early += [functools.partial(chain, sums, 2 * pair + i, t) for t in (0, 3)]
+        late += [functools.partial(chain, sums, 2 * pair + i, t) for t in (1, 2)]
+        late.append(functools.partial(finish, sums, i))
+    return early, late
+
+
+def conv_rows(*args):
     for i in range(2):
-        sums = []
-        for t in range(4):
-            steps.append(functools.partial(chain, sums, 2 * pair + i, t))
-        steps.append(functools.partial(finish, sums, i))
-    return steps
-
-
-def conv_rows(*args):
-    for step in conv_steps(*args):
-        step()
+        early, late = conv_steps(*args, parts=(i,))
+        for step in early + late:
+            step()
 
 
 def interleave(matrix_steps, vector_steps):

time: 44.9 us -> 44.5 us (level)
  no operation moved by 1% of the time
where the time goes in v3:
time: 44.5 us; the launch traced here: 44.3 us
  Pallas kernels  27.5 us (62%)
  starting transfers between devices  10.7 us (24%)
  waiting for transfers between devices  5.8 us (13%)
    pallas_call x9, Pallas kernels, call(): pl.pallas_call(kernel, out_shape=outs, in_specs=[pl.BlockSpec(memory_spac...  27.5 us
    ppermute x2, starting transfers between devices, exchange(): far = lax.ppermute(far, 'rows', routes[1])  6.06 us
    ppermute x1, waiting for transfers between devices, on_device(): outer = lax.ppermute(outer, 'tm', chain('tm', WRAPS[2]))  4.22 us
    ppermute x1, starting transfers between devices, on_device(): inner = lax.ppermute(inner, 'tm', chain('tm', WRAPS[1]))  1.86 us
    ppermute x1, waiting for transfers between devices, on_device(): carried = lax.ppermute(carry, 'tm', chain('tm', WRAPS[0]))  1.41 us
    ppermute x1, starting transfers between devices, on_device(): outer = lax.ppermute(outer, 'tm', chain('tm', WRAPS[2]))  1.29 us
    ppermute x2, starting transfers between devices, exchange(): near = lax.ppermute(near, 'rows', routes[0])  1.2 us
  transfers between devices with their start and end apart: 7, of which 3 were waited for; matrix products, arithmetic and copies ran while one was open for 0% of the time, Pallas kernels for 51%

profile of v3, /device:TPU:27, one launch (start us, length us, event | category | flops | bytes accessed | tf_op | source)
XLA Modules:
  0.0 44.3 jit_solution(5054363015987410895)
XLA Ops:
  0.0 1.3 %shard_map.82 = (bf16[4,1,128,256]{3,2,1,0:T(8,128)(2,1)S(1)}, bf16[4,1,128,256]{3,2,1,0:T(8,128)(2,1)S(1)}, bf16[1,8,128,256]{3,2,1,0:T(8,128)(2,1)S(1)}, f32[1,256]{1,0:T(1,128)S(1)}) custom-call(bf16[4,8,128,256]{3,2,1,0:T(8,128)(2,1)} %feat_hbm.3, f32[1,256]{1,0:T(1,128)} %bitcast.14), custom_call_target="tpu_custom_call" | custom-call | bytes 2098176 | tf_op jit(solution)/shard_map/pallas_call | solution.py:26
  1.3 0.7 %collective-permute-start = (bf16[4,1,128,256]{3,2,1,0:T(8,128)(2,1)S(1)}, bf16[4,1,128,256]{3,2,1,0:T(8,128)(2,1)S(1)}, u32[]{:S(2)}, u32[]{:S(2)}) collective-permute-start(bf16[4,1,128,256]{3,2,1,0:T(8,128)(2,1)S(1)} %get-tuple-element.28), channel_id=1, source_target_pairs={{0,1},{1,0},{2,3},{3,2},{4,5},{5,4},{6,7},{7,6},{8,9},{9,8},{10,11... | collective-permute-start | bytes 786440 | tf_op jit(solution)/shard_map/ppermute | solution.py:487
  2.0 3.0 %collective-permute-start.1 = (bf16[4,1,128,256]{3,2,1,0:T(8,128)(2,1)S(1)}, bf16[4,1,128,256]{3,2,1,0:T(8,128)(2,1)S(1)}, u32[]{:S(2)}, u32[]{:S(2)}) collective-permute-start(bf16[4,1,128,256]{3,2,1,0:T(8,128)(2,1)S(1)} %get-tuple-element.29), channel_id=1, source_target_pairs={{0,0},{1,2},{2,1},{3,4},{4,3},{5,6},{6,5},{7,7},{8,8},{9,10},{10,9... | collective-permute-start | bytes 786440 | tf_op jit(solution)/shard_map/ppermute | solution.py:488
  5.0 7.7 %shard_map.83 = (bf16[4,4,10,64,256]{4,3,2,1,0:T(8,128)(2,1)S(1)}, f32[4,2,8,64,256]{4,3,2,1,0:T(8,128)S(1)}, bf16[8,256,512]{2,1,0:T(8,128)(2,1)S(1)}, bf16[3,3...) custom-call(bf16[1,8,128,256]{3,2,1,0:T(8,128)(2,1)S(1)} %get-tuple-, ...), custom_call_target="tpu_custom_call" | custom-call | flops 5000000000 | bytes 8258560 | tf_op jit(solution)/shard_map/pallas_call | solution.py:26
  12.8 0.0 collective-permute-done.near_ref
  12.8 0.0 collective-permute-done.1.far_ref
  12.8 0.0 copy-start
  12.8 0.0 copy-start.1
  12.8 0.0 copy-start.2
  12.8 2.4 %shard_map.84 = (bf16[4,4,10,64,256]{4,3,2,1,0:T(8,128)(2,1)S(1)}, bf16[8,4,64,256]{3,2,1,0:T(8,128)(2,1)S(1)}, bf16[4,64,512]{2,1,0:T(8,128)(2,1)S(1)}) custom-call(bf16[4,4,10,64,256]{4,3,2,1,0:T(8,128)(2,1)S(1)} %get-tuple-element.26.x_in, bf16[8,4,64,256]{3,2,1,0:T(8,128)(2,1)S(1)} %get-tuple-element.27.lev_in, ...), custom_call_target="tpu_custom_call", output_to_operand_aliasing={{0}: (0, {}), {1}: (1, {})} | custom-call | flops 2952790016 | bytes 14812160 | tf_op jit(solution)/shard_map/pallas_call | solution.py:26
  15.2 0.2 collective-permute-start.2
  15.4 0.0 slice-start
  15.4 0.0 copy-done
  15.4 0.0 copy-done.1
  15.5 0.0 copy-done.2
  15.5 0.0 slice-start.1
  15.5 0.0 slice-start.2
  15.5 0.0 slice-start.3
  15.5 6.8 %shard_map.85 = (bf16[8,4,64,256]{3,2,1,0:T(8,128)(2,1)S(1)}, f32[4,64,512]{2,1,0:T(8,128)S(1)}, f32[4,64,512]{2,1,0:T(8,128)S(1)}, bf16[4,64,512]{2,1,0:T(8,128)(2,1)S(1)}) custom-call(bf16[8,4,64,256]{3,2,1,0:T(8,128)(2,1)S(1)} %get-tuple-element.25.lev_in, ...), custom_call_target="tpu_custom_call", output_to_operand_aliasing={{0}: (0, {})} | custom-call | flops 8321499136 | bytes 18532352 | tf_op jit(solution)/shard_map/pallas_call | solution.py:26
  22.3 1.4 %collective-permute-done.2.carried_ref = bf16[4,64,512]{2,1,0:T(8,128)(2,1)S(1)} collective-permute-done((bf16[4,64,512]{2,1,0:T(8,128)(2,1)S(1)}, bf16[4,64,512]{2,1,0:T(8,128)(2,1)S(1)}, u32[]{:S(2)}, u32[]{:S(2)}) %collective-permute-start.2) | collective-permute-done | bytes 262176 | tf_op jit(solution)/shard_map/ppermute | solution.py:560
  23.7 0.3 shard_map.86
  24.1 0.5 %collective-permute-start.3 = (bf16[2,1,64,512]{3,2,1,0:T(8,128)(2,1)S(1)}, bf16[2,1,64,512]{3,2,1,0:T(8,128)(2,1)S(1)}, u32[]{:S(2)}, u32[]{:S(2)}) collective-permute-start(bf16[2,1,64,512]{3,2,1,0:T(8,128)(2,1)S(1)} %get-tuple-element.42), channel_id=1, source_target_pairs={{0,1},{1,0},{2,3},{3,2},{4,5},{5,4},{6,7},{7,6},{8,9},{9,8},{10,11... | collective-permute-start | bytes 393224 | tf_op jit(solution)/shard_map/ppermute | solution.py:487
  24.5 3.0 %collective-permute-start.4 = (bf16[2,1,64,512]{3,2,1,0:T(8,128)(2,1)S(1)}, bf16[2,1,64,512]{3,2,1,0:T(8,128)(2,1)S(1)}, u32[]{:S(2)}, u32[]{:S(2)}) collective-permute-start(bf16[2,1,64,512]{3,2,1,0:T(8,128)(2,1)S(1)} %get-tuple-element.41), channel_id=1, source_target_pairs={{0,0},{1,2},{2,1},{3,4},{4,3},{5,6},{6,5},{7,7},{8,8},{9,10},{10,9... | collective-permute-start | bytes 393224 | tf_op jit(solution)/shard_map/ppermute | solution.py:488
  27.6 0.0 slice-done
  27.6 0.0 slice-done.1
  27.6 0.0 slice-done.2
  27.6 0.0 slice-done.3
  27.6 2.1 %shard_map.88 = bf16[2,2,64,512]{3,2,1,0:T(8,128)(2,1)S(1)} custom-call(bf16[4,64,512]{2,1,0:T(8,128)(2,1)S(1)} %get-tuple-element.37.refs_0_.before_ref, bf16[4,64,512]{2,1,0:T(8,128)(2,1)S(1)} %get-tuple-element.38.refs_1_.latest_ref, bf16[3,3,3,512,512]{4,3,2,1,0:T(8,128)(2,1)S(1)} %bitcast.11), custom_call_target="tpu_custom_call" | custom-call | flops 1811939328 | bytes 14680064 | tf_op jit(solution)/shard_map/pallas_call | solution.py:26
  29.7 1.9 %collective-permute-start.5 = (bf16[2,2,64,512]{3,2,1,0:T(8,128)(2,1)S(1)}, bf16[2,2,64,512]{3,2,1,0:T(8,128)(2,1)S(1)}, u32[]{:S(2)}, u32[]{:S(2)}) collective-permute-start(bf16[2,2,64,512]{3,2,1,0:T(8,128)(2,1)S(1)} %shard_map.88), channel_id=1, source_target_pairs={{0,8},{8,16},{16,24},{24,0},{1,9},{9,17},{17,25},{25,1},{2,10},{10... | collective-permute-start | bytes 786440 | tf_op jit(solution)/shard_map/ppermute | solution.py:596
  31.6 0.0 collective-permute-done.3.refs_4_.near_ref
  31.6 0.1 collective-permute-done.4.refs_5_.far_ref
  31.7 2.1 %shard_map.89 = bf16[2,2,64,512]{3,2,1,0:T(8,128)(2,1)S(1)} custom-call(bf16[4,64,512]{2,1,0:T(8,128)(2,1)S(1)} %get-tuple-element.37.refs_0_.before_ref, bf16[4,64,512]{2,1,0:T(8,128)(2,1)S(1)} %get-tuple-element.38.refs_1_.latest_ref, bf16[2,1,64,512]{3,2,1,0:T(8,128)(2,1)S(1)} %collective-permute-done.3.refs_4_.near_ref, ...), custom_call_target="tpu_custom_call" | custom-call | flops 1811939328 | bytes 14942208 | tf_op jit(solution)/shard_map/pallas_call | solution.py:26
  33.8 1.3 %collective-permute-start.6 = (bf16[2,2,64,512]{3,2,1,0:T(8,128)(2,1)S(1)}, bf16[2,2,64,512]{3,2,1,0:T(8,128)(2,1)S(1)}, u32[]{:S(2)}, u32[]{:S(2)}) collective-permute-start(bf16[2,2,64,512]{3,2,1,0:T(8,128)(2,1)S(1)} %shard_map.89), channel_id=1, source_target_pairs={{0,8},{8,16},{16,24},{1,9},{9,17},{17,25},{2,10},{10,18},{18,26},{... | collective-permute-start | bytes 786440 | tf_op jit(solution)/shard_map/ppermute | solution.py:604
  35.1 4.1 %shard_map.87.own_ref = f32[2,4,64,512]{3,2,1,0:T(8,128)S(1)} custom-call(bf16[4,64,512]{2,1,0:T(8,128)(2,1)S(1)} %get-tuple-element.37.refs_0_.before_ref, bf16[4,64,512]{2,1,0:T(8,128)(2,1)S(1)} %get-tuple-element.38.refs_1_.latest_ref, f32[4,64,512]{2,1,0:T(8,128)S(1)} %get-tuple-element.39.refs_2_, f32[4,64,512]{2,1,0:T(8,128)S(1)} %get-tuple-element.40.refs_3_, ...), custom_call_target="tpu_custom_call" | custom-call | flops 3623878656 | bytes 15990784 | tf_op jit(solution)/shard_map/pallas_call | solution.py:26
  39.2 0.0 collective-permute-done.5.inner_ref
  39.2 4.2 %collective-permute-done.6.outer_ref = bf16[2,2,64,512]{3,2,1,0:T(8,128)(2,1)S(1)} collective-permute-done((bf16[2,2,64,512]{3,2,1,0:T(8,128)(2,1)S(1)}, bf16[2,2,64,512]{3,2,1,0:T(8,128)(2,1)S(1)}, u32[]{:S(2)}, u32[]{:S(2)}) %collective-permute-start.6) | collective-permute-done | bytes 262176 | tf_op jit(solution)/shard_map/ppermute | solution.py:604
  43.4 0.9 %shard_map.90 = bf16[2,4,64,512]{3,2,1,0:T(8,128)(2,1)} custom-call(f32[2,4,64,512]{3,2,1,0:T(8,128)S(1)} %shard_map.87.own_ref, bf16[2,2,64,512]{3,2,1,0:T(8,128)(2,1)S(1)} %collective-permute-done.5.inner_ref, bf16[2,2,64,512]{3,2,1,0:T(8,128)(2,1)S(1)} %collective-permute-done.6.outer_ref), custom_call_target="tpu_custom_call" | custom-call | bytes 1572864 | tf_op jit(solution)/shard_map/pallas_call | solution.py:26
  (3 shorter events, 0.1 us)
Async XLA Ops:
  1.3 11.5 %collective-permute-start = (bf16[4,1,128,256]{3,2,1,0:T(8,128)(2,1)S(1)}, bf16[4,1,128,256]{3,2,1,0:T(8,128)(2,1)S(1)}, u32[]{:S(2)}, u32[]{:S(2)}) collective-permute-start(bf16[4,1,128,256]{3,2,1,0:T(8,128)(2,1)S(1)} %get-tuple-element.28), channel_id=1, source_target_pairs={{0,1},{1,0},{2,3},{3,2},{4,5},{5,4},{6,7},{7,6},{8,9},{9,8},{10,11... | collective-permute-start | bytes 786440 | tf_op jit(solution)/shard_map/ppermute | solution.py:487
  2.0 10.8 %collective-permute-start.1 = (bf16[4,1,128,256]{3,2,1,0:T(8,128)(2,1)S(1)}, bf16[4,1,128,256]{3,2,1,0:T(8,128)(2,1)S(1)}, u32[]{:S(2)}, u32[]{:S(2)}) collective-permute-start(bf16[4,1,128,256]{3,2,1,0:T(8,128)(2,1)S(1)} %get-tuple-element.29), channel_id=1, source_target_pairs={{0,0},{1,2},{2,1},{3,4},{4,3},{5,6},{6,5},{7,7},{8,8},{9,10},{10,9... | collective-permute-start | bytes 786440 | tf_op jit(solution)/shard_map/ppermute | solution.py:488
  12.8 2.7 %copy-start = (f32[512]{0:T(512)S(1)}, f32[512]{0:T(512)}, u32[]{:S(2)}) copy-start(f32[512]{0:T(512)} %param.14) | copy-start | bytes 6148
  12.8 2.7 %copy-start.1 = (bf16[2,24,4,64]{3,2,1,0:T(4,128)(2,1)S(1)}, bf16[2,24,4,64]{3,2,1,0:T(4,128)(2,1)}, u32[]{:S(2)}) copy-start(bf16[2,24,4,64]{3,2,1,0:T(4,128)(2,1)} %wav_ref.1) | copy-start | bytes 73732
  12.8 2.7 %copy-start.2 = (bf16[24,512]{1,0:T(8,128)(2,1)S(1)}, bf16[24,512]{1,0:T(8,128)(2,1)}, u32[]{:S(2)}) copy-start(bf16[24,512]{1,0:T(8,128)(2,1)} %inj_ref.1) | copy-start | bytes 73732
  15.2 8.5 %collective-permute-start.2 = (bf16[4,64,512]{2,1,0:T(8,128)(2,1)S(1)}, bf16[4,64,512]{2,1,0:T(8,128)(2,1)S(1)}, u32[]{:S(2)}, u32[]{:S(2)}) collective-permute-start(bf16[4,64,512]{2,1,0:T(8,128)(2,1)S(1)} %get-tuple-element.36), channel_id=1, source_target_pairs={{0,8},{8,16},{16,24},{24,0},{1,9},{9,17},{17,25},{25,1},{2,10},{10... | collective-permute-start | bytes 786440 | tf_op jit(solution)/shard_map/ppermute | solution.py:560
  15.4 12.2 %slice-start = ((s8[14155776]{0:T(1024)(128)(4,1)}), s8[4194304]{0:T(1024)(128)(4,1)S(1)}, s32[]{:S(2)}) async-start(s8[14155776]{0:T(1024)(128)(4,1)} %bitcast.10), calls=%async_computation | async-start | bytes 8388608
  15.5 12.1 %slice-start.1 = ((s8[14155776]{0:T(1024)(128)(4,1)}), s8[4194304]{0:T(1024)(128)(4,1)S(1)}, s32[]{:S(2)}) async-start(s8[14155776]{0:T(1024)(128)(4,1)} %bitcast.10), calls=%async_computation.1 | async-start | bytes 8388608
  15.5 12.1 %slice-start.2 = ((s8[14155776]{0:T(1024)(128)(4,1)}), s8[4194304]{0:T(1024)(128)(4,1)S(1)}, s32[]{:S(2)}) async-start(s8[14155776]{0:T(1024)(128)(4,1)} %bitcast.10), calls=%async_computation.2 | async-start | bytes 8388608
  15.5 12.1 %slice-start.3 = ((s8[14155776]{0:T(1024)(128)(4,1)}), s8[1572864]{0:T(1024)(128)(4,1)S(1)}, s32[]{:S(2)}) async-start(s8[14155776]{0:T(1024)(128)(4,1)} %bitcast.10), calls=%async_computation.3 | async-start | bytes 3145728
  24.1 7.5 %collective-permute-start.3 = (bf16[2,1,64,512]{3,2,1,0:T(8,128)(2,1)S(1)}, bf16[2,1,64,512]{3,2,1,0:T(8,128)(2,1)S(1)}, u32[]{:S(2)}, u32[]{:S(2)}) collective-permute-start(bf16[2,1,64,512]{3,2,1,0:T(8,128)(2,1)S(1)} %get-tuple-element.42), channel_id=1, source_target_pairs={{0,1},{1,0},{2,3},{3,2},{4,5},{5,4},{6,7},{7,6},{8,9},{9,8},{10,11... | collective-permute-start | bytes 393224 | tf_op jit(solution)/shard_map/ppermute | solution.py:487
  24.5 7.2 %collective-permute-start.4 = (bf16[2,1,64,512]{3,2,1,0:T(8,128)(2,1)S(1)}, bf16[2,1,64,512]{3,2,1,0:T(8,128)(2,1)S(1)}, u32[]{:S(2)}, u32[]{:S(2)}) collective-permute-start(bf16[2,1,64,512]{3,2,1,0:T(8,128)(2,1)S(1)} %get-tuple-element.41), channel_id=1, source_target_pairs={{0,0},{1,2},{2,1},{3,4},{4,3},{5,6},{6,5},{7,7},{8,8},{9,10},{10,9... | collective-permute-start | bytes 393224 | tf_op jit(solution)/shard_map/ppermute | solution.py:488
  29.7 9.5 %collective-permute-start.5 = (bf16[2,2,64,512]{3,2,1,0:T(8,128)(2,1)S(1)}, bf16[2,2,64,512]{3,2,1,0:T(8,128)(2,1)S(1)}, u32[]{:S(2)}, u32[]{:S(2)}) collective-permute-start(bf16[2,2,64,512]{3,2,1,0:T(8,128)(2,1)S(1)} %shard_map.88), channel_id=1, source_target_pairs={{0,8},{8,16},{16,24},{24,0},{1,9},{9,17},{17,25},{25,1},{2,10},{10... | collective-permute-start | bytes 786440 | tf_op jit(solution)/shard_map/ppermute | solution.py:596
  33.8 9.6 %collective-permute-start.6 = (bf16[2,2,64,512]{3,2,1,0:T(8,128)(2,1)S(1)}, bf16[2,2,64,512]{3,2,1,0:T(8,128)(2,1)S(1)}, u32[]{:S(2)}, u32[]{:S(2)}) collective-permute-start(bf16[2,2,64,512]{3,2,1,0:T(8,128)(2,1)S(1)} %shard_map.89), channel_id=1, source_target_pairs={{0,8},{8,16},{16,24},{1,9},{9,17},{17,25},{2,10},{10,18},{18,26},{... | collective-permute-start | bytes 786440 | tf_op jit(solution)/shard_map/ppermute | solution.py:604
